TPU v7x, 32 devices: a whole 2x2x4 slice. The times are simulated.
32 devices in a mesh: mx: 4 (over z), my: 4 (over y, core), col: 2 (over x).
Axes of the slice: x: 2, y: 2, z: 4, core: 2. Of those that a mesh axis runs over, the one named last changes fastest.
Arguments:
- spectrum: float32 [2, 4, 128, 32, 512], P(None, 'col', None, 'mx', 'my'), may hold values from -6 to 6
- core_tensor: float32 [2, 64, 64, 16, 16, 16], P(None, 'col', None, ('mx', 'my')), may hold values from -0.01171875 to 0.01171875
- input_factor: float32 [128, 64], replicated, may hold values from -0.5 to 0.5
- output_factor: float32 [128, 64], replicated, may hold values from -0.75 to 0.75
- first_factor: float32 [32, 16], P('mx'), may hold values from -5 to 5
- second_factor: float32 [32, 16], P('my'), may hold values from -5 to 5
- third_factor: float32 [16, 16], replicated, may hold values from -5 to 5
Outputs:
- mixed_modes: float32 [2, 4, 128, 32, 512], P(None, 'col', None, 'mx', 'my')
All inputs are finite; a program needn't handle non-finite values.
Results may differ from a plain program's by a relative error of at most 0.00007.
Values sent between devices are 32-bit elements; how exact they have to be, the bound alone decides.
A program may use at most 192 MiB of HBM per device.

v0:
```python
import functools

import jax
import jax.numpy as jnp
from jax import lax
from jax.experimental import pallas as pl
from jax.experimental.pallas import tpu as pltpu
from jax.sharding import PartitionSpec as P

MESH = pl.DeviceIdType.MESH
F32 = jnp.float32
BF16 = jnp.bfloat16


def halves(value):
    high = value.astype(BF16)
    return high, (value - high.astype(F32)).astype(BF16)


def dot_split(left, right):
    (lh, ll), (rh, rl) = left, right
    dot = functools.partial(jnp.dot, preferred_element_type=F32)
    return dot(lh, rh) + (dot(lh, rl) + dot(ll, rh))


def whole_div(x, n):
    assert n & (n - 1) == 0
    return x >> (n.bit_length() - 1)


def whole_rem(x, n):
    assert n & (n - 1) == 0
    return x & (n - 1)


def iota(shape, dim):
    return lax.broadcasted_iota(jnp.int32, shape, dim)


def picks_rows(count, width, pick):
    return (pick(iota((count, width), 0)) == iota((count, width), 1)).astype(F32)


def picks_columns(width, count, pick):
    return (iota((width, count), 0) == pick(iota((width, count), 1))).astype(F32)


exact = functools.partial(
    lax.dot_general, precision=lax.Precision.HIGHEST, preferred_element_type=F32
)
PLAIN = (((1,), (0,)), ((), ()))
TURNED = (((1,), (1,)), ((), ()))


def kernel(
    dims,
    spec_ref, core_hbm, ift_ref, of_ref, first_ref, second_ref, third_ref,
    out_ref,
    core_v, xs, X, T, S, E, G, Y, R, W, F1, F2, kbig, ktu_s, kf1_s,
    core_sem, fsend, frecv, hsend, hrecv,
    xsend, xrecv, tsend, trecv, esend, erecv, ysend, yrecv,
):
    nx, ny, nc, chunks, pc, group, r4, r5 = dims
    n_s = nx * ny
    mx, my, col = lax.axis_index("mx"), lax.axis_index("my"), lax.axis_index("col")
    b_loc, cin, kx_loc, lanes = spec_ref.shape[1:]
    q_loc = G.shape[5]
    q_all = core_hbm.shape[3]
    p_all = ift_ref.shape[0]
    cout = out_ref.shape[2]
    ky_loc = second_ref.shape[0]
    r3 = n_s
    modes_third = third_ref.shape[0]

    def side(d):
        return lax.rem(mx + d // nc, nx), lax.rem(col + d % nc, nc)

    def side_from(d):
        return lax.rem(mx + nx - d // nc, nx), lax.rem(col + nc - d % nc, nc)

    def each(low, high, act):
        def step(d, _):
            act(d)
            return 0

        lax.fori_loop(low, high, step, 0)

    def send(src, dst, send_sem, recv_sem, a, b, c):
        return pltpu.make_async_remote_copy(
            src_ref=src, dst_ref=dst, send_sem=send_sem, recv_sem=recv_sem,
            device_id=(a, b, c), device_id_type=MESH,
        )

    core_copy = pltpu.make_async_copy(core_hbm, core_v, core_sem)
    core_copy.start()

    barrier = pltpu.get_barrier_semaphore()

    def tell(a, b, c):
        pl.semaphore_signal(barrier, inc=1, device_id=(a, b, c), device_id_type=MESH)

    each(1, nx * nc, lambda d: tell(side(d)[0], my, side(d)[1]))
    each(1, ny, lambda d: tell(mx, lax.rem(my + d, ny), col))

    def first_copy(d):
        return send(first_ref, F1.at[mx], fsend.at[d], frecv.at[d], lax.rem(mx + d, nx), my, col)

    def first_arrival(d):
        a = lax.rem(mx + nx - d, nx)
        return send(first_ref, F1.at[a], fsend.at[d], frecv.at[d], a, my, col)

    def second_copy(d):
        return send(second_ref, F2.at[my], hsend.at[d], hrecv.at[d], mx, lax.rem(my + d, ny), col)

    def second_arrival(d):
        b = lax.rem(my + ny - d, ny)
        return send(second_ref, F2.at[b], hsend.at[d], hrecv.at[d], mx, b, col)

    def x_copy(k, d):
        a, c = side(d)
        return send(xs.at[k, c], X.at[k, mx, col], xsend.at[k, d], xrecv.at[k, d], a, my, c)

    def x_arrival(k, d):
        a, c = side_from(d)
        return send(xs.at[k, c], X.at[k, a, c], xsend.at[k, d], xrecv.at[k, d], a, my, c)

    def t_copy(k, d):
        a = lax.rem(mx + d, nx)
        return send(T.at[k, a], S.at[k, mx], tsend.at[k, d], trecv.at[k, d], a, my, col)

    def t_arrival(k, d):
        a = lax.rem(mx + nx - d, nx)
        return send(T.at[k, mx], S.at[k, a], tsend.at[k, d], trecv.at[k, d], a, my, col)

    def e_copy(k, d):
        b = lax.rem(my + d, ny)
        return send(E.at[k, b], G.at[k, my], esend.at[k, d], erecv.at[k, d], mx, b, col)

    def e_arrival(k, d):
        b = lax.rem(my + ny - d, ny)
        return send(E.at[k, my], G.at[k, b], esend.at[k, d], erecv.at[k, d], mx, b, col)

    def y_copy(d):
        a, c = side(d)
        return send(Y.at[a, c], R.at[mx, col], ysend.at[d], yrecv.at[d], a, my, c)

    def y_arrival(d):
        a, c = side_from(d)
        return send(Y.at[mx, col], R.at[a, c], ysend.at[d], yrecv.at[d], a, my, c)

    def expand_factor(factor):
        rows, columns = factor.shape
        n, m = rows * kx_loc, columns * kx_loc
        full = exact(
            exact(picks_rows(n, rows, lambda r: whole_div(r, kx_loc)), factor, PLAIN),
            picks_columns(columns, m, lambda j: whole_div(j, kx_loc)),
            PLAIN,
        )
        same = whole_rem(iota((n, m), 0), kx_loc) == whole_rem(iota((n, m), 1), kx_loc)
        high, low = halves(jnp.where(same, full, 0.0))
        return high, low

    pl.semaphore_wait(barrier, nx * nc - 1 + ny - 1)
    each(1, nx, lambda d: first_copy(d).start())
    each(1, ny, lambda d: second_copy(d).start())
    F1[mx] = first_ref[...]
    F2[my] = second_ref[...]
    core_copy.wait()

    for k in range(chunks):
        for c in range(2):
            def turn(i, _):
                block = core_v[c, k * pc + i].T
                for a in range(nx):
                    T[k, a, c, i] = block[a * q_loc : (a + 1) * q_loc]
                return 0

            lax.fori_loop(0, pc, turn, 0)
        each(1, nx, lambda d: t_copy(k, d).start())
        S[k, mx] = T[k, mx]

    h, l = expand_factor(ift_ref[...])
    kbig[0], kbig[1] = h, l
    for b in range(b_loc):
        right = jnp.concatenate(
            [spec_ref[c, b].reshape(cin * kx_loc, lanes) for c in range(2)], axis=1
        )
        got = dot_split((kbig[0], kbig[1]), halves(right))
        for c in range(2):
            piece = got[:, c * lanes : (c + 1) * lanes]
            piece = piece.reshape(nc, chunks, pc, kx_loc, lanes)
            for k in range(chunks):
                xs[k, :, c, b] = piece[:, k]
    for k in range(chunks):
        each(1, nx * nc, lambda d: x_copy(k, d).start())
        X[k, mx, col] = xs[k, col]

    each(1, nx, lambda d: first_arrival(d).wait_recv())
    each(1, ny, lambda d: second_arrival(d).wait_recv())
    wide = F1.shape[2]
    n, m = nx * q_loc * kx_loc, n_s * q_loc
    full = exact(
        exact(
            picks_rows(
                n, nx * kx_loc,
                lambda r: whole_div(r, q_loc * kx_loc) * kx_loc + whole_rem(r, kx_loc),
            ),
            F1[...].reshape(nx * kx_loc, wide),
            PLAIN,
        ),
        picks_columns(
            wide, m,
            lambda j: whole_rem(whole_div(j, q_loc), nx) * ny + whole_div(j, q_loc * nx),
        ),
        PLAIN,
    )
    same = whole_rem(whole_div(iota((n, m), 0), kx_loc), q_loc) == whole_rem(
        iota((n, m), 1), q_loc
    )
    h, l = halves(jnp.where(same, full, 0.0))
    kf1_s[0], kf1_s[1] = h, l
    n, m = r4 * r5, ny * lanes
    by_second = exact(
        exact(
            picks_rows(n, wide, lambda r: whole_div(r, r5)),
            F2[...].reshape(ny * ky_loc, wide),
            TURNED,
        ),
        picks_columns(ny * ky_loc, m, lambda j: whole_div(j, modes_third)),
        PLAIN,
    )
    by_third = exact(
        exact(picks_rows(n, wide, lambda r: whole_rem(r, r5)), third_ref[...], TURNED),
        picks_columns(modes_third, m, lambda j: whole_rem(j, modes_third)),
        PLAIN,
    )
    h, l = halves(by_second * by_third)
    ktu_s[0], ktu_s[1] = h, l

    for k in range(chunks):
        each(1, nx, lambda d: t_arrival(k, d).wait_recv())
        for c in range(2):
            def expand(g, _):
                base = g * group
                left = jnp.concatenate(
                    [S[k, :, c, base + i].reshape(q_all, r4 * r5) for i in range(group)],
                    axis=0,
                )
                got = dot_split(halves(left), (ktu_s[0], ktu_s[1]))
                for i in range(group):
                    for b in range(ny):
                        E[k, b, :, c, base + i] = got[
                            i * q_all : (i + 1) * q_all, b * lanes : (b + 1) * lanes
                        ].reshape(nx, q_loc, lanes)
                return 0

            lax.fori_loop(0, pc // group, expand, 0)
        each(1, ny, lambda d: e_copy(k, d).start())
        G[k, my] = E[k, my]

    for k in range(chunks):
        each(1, ny, lambda d: e_arrival(k, d).wait_recv())
        for g in range(pc // group):
            first = k == 0 and g == 0

            def weigh(i, _):
                right = jnp.concatenate(
                    [
                        G[k, :, :, c, g * group + i].reshape(n_s * q_loc, lanes)
                        for c in range(2)
                    ],
                    axis=1,
                )
                got = dot_split((kf1_s[0], kf1_s[1]), halves(right))
                got = got.reshape(nx, q_loc, kx_loc, 2 * lanes)
                W[i, :, 0] = got[..., :lanes]
                W[i, :, 1] = got[..., lanes:]
                return 0

            lax.fori_loop(0, group, weigh, 0)
            if g == 0:
                each(1, nx * nc, lambda d: x_arrival(k, d).wait_recv())

            def add_up(j, _):
                a, rest = j // (nc * b_loc), j % (nc * b_loc)
                s, b = rest // b_loc, rest % b_loc
                real = imag = None
                for i in range(group):
                    p = g * group + i
                    xr, xi = X[k, a, s, 0, b, p], X[k, a, s, 1, b, p]
                    wr, wi = W[i, a, 0], W[i, a, 1]
                    re = xr * wr - xi * wi
                    im = xr * wi + xi * wr
                    real = re if real is None else real + re
                    imag = im if imag is None else imag + im
                if first:
                    Y[a, s, 0, b] = real
                    Y[a, s, 1, b] = imag
                else:
                    Y[a, s, 0, b] += real
                    Y[a, s, 1, b] += imag
                return 0

            lax.fori_loop(0, nx * nc * b_loc, add_up, 0)

    each(1, nx * nc, lambda d: y_copy(d).start())
    R[mx, col] = Y[mx, col]
    kout = expand_factor(of_ref[...])
    each(1, nx, lambda d: first_copy(d).wait_send())
    each(1, ny, lambda d: second_copy(d).wait_send())
    for k in range(chunks):
        each(1, nx * nc, lambda d: x_copy(k, d).wait_send())
        each(1, nx, lambda d: t_copy(k, d).wait_send())
        each(1, ny, lambda d: e_copy(k, d).wait_send())
    each(1, nx * nc, lambda d: y_arrival(d).wait_recv())

    for b in range(b_loc):
        columns = []
        for c in range(2):
            total = R[:, 0, c, b]
            for s in range(1, nc):
                total = total + R[:, s, c, b]
            columns.append(total.reshape(q_all * kx_loc, lanes))
        got = dot_split(kout, halves(jnp.concatenate(columns, axis=1)))
        for c in range(2):
            out_ref[c, b] = got[:, c * lanes : (c + 1) * lanes].reshape(
                cout, kx_loc, lanes
            )
    each(1, nx * nc, lambda d: y_copy(d).wait_send())


def per_device(
    nx, ny, nc,
    spectrum, core_tensor, input_factor, output_factor, first_factor, second_factor, third_factor,
):
    _, b_loc, cin, kx_loc, lanes = spectrum.shape
    _, p_loc, q_all, _, r4, r5 = core_tensor.shape
    p_all = input_factor.shape[1]
    cout = output_factor.shape[0]
    n_s = nx * ny
    q_loc = q_all // nx
    chunks = 4
    pc = p_loc // chunks
    group = 4 if pc % 4 == 0 else pc

    def widen(factor):
        return jnp.pad(factor, ((0, 0), (0, lanes - factor.shape[1])))

    core = jnp.transpose(core_tensor, (0, 1, 3, 4, 5, 2)).reshape(2, p_loc, r4 * r5, q_all)
    ky_loc = second_factor.shape[0]
    tu, m_all = r4 * r5, ny * lanes
    vmem = pl.BlockSpec(memory_space=pltpu.VMEM)
    dma = pltpu.SemaphoreType.DMA
    return pl.pallas_call(
        functools.partial(kernel, (nx, ny, nc, chunks, pc, group, r4, r5)),
        out_shape=jax.ShapeDtypeStruct((2, b_loc, cout, kx_loc, lanes), F32),
        in_specs=[vmem, pl.BlockSpec(memory_space=pl.ANY)] + [vmem] * 5,
        out_specs=vmem,
        scratch_shapes=[
            pltpu.VMEM(core.shape, F32),
            pltpu.VMEM((chunks, nc, 2, b_loc, pc, kx_loc, lanes), F32),
            pltpu.VMEM((chunks, nx, nc, 2, b_loc, pc, kx_loc, lanes), F32),
            pltpu.VMEM((chunks, nx, 2, pc, q_loc, tu), F32),
            pltpu.VMEM((chunks, nx, 2, pc, q_loc, tu), F32),
            pltpu.VMEM((chunks, ny, nx, 2, pc, q_loc, lanes), F32),
            pltpu.VMEM((chunks, ny, nx, 2, pc, q_loc, lanes), F32),
            pltpu.VMEM((nx, nc, 2, b_loc, q_loc, kx_loc, lanes), F32),
            pltpu.VMEM((nx, nc, 2, b_loc, q_loc, kx_loc, lanes), F32),
            pltpu.VMEM((group, nx, 2, q_loc, kx_loc, lanes), F32),
            pltpu.VMEM((nx, kx_loc, lanes), F32),
            pltpu.VMEM((ny, ky_loc, lanes), F32),
            pltpu.VMEM((2, p_all * kx_loc, cin * kx_loc), BF16),
            pltpu.VMEM((2, tu, m_all), BF16),
            pltpu.VMEM((2, nx * q_loc * kx_loc, n_s * q_loc), BF16),
            dma,
            dma((nx,)), dma((nx,)), dma((ny,)), dma((ny,)),
            dma((chunks, nx * nc)), dma((chunks, nx * nc)),
            dma((chunks, nx)), dma((chunks, nx)),
            dma((chunks, ny)), dma((chunks, ny)),
            dma((nx * nc,)), dma((nx * nc,)),
        ],
        compiler_params=pltpu.CompilerParams(
            collective_id=0, has_side_effects=True, vmem_limit_bytes=61000 * 1024
        ),
    )(
        spectrum, core, input_factor.T, output_factor,
        widen(first_factor), widen(second_factor), widen(third_factor),
    )


def solution(mesh):
    placed = (
        P(None, "col", None, "mx", "my"),
        P(None, "col", None, ("mx", "my"), None, None),
        P(),
        P(),
        P("mx", None),
        P("my", None),
        P(),
    )
    return jax.shard_map(
        functools.partial(
            per_device, mesh.shape["mx"], mesh.shape["my"], mesh.shape["col"]
        ),
        mesh=mesh,
        in_specs=placed,
        out_specs=P(None, "col", None, "mx", "my"),
        check_vma=False,
    )
```

profile of v0, /device:TPU:28, one launch (start us, length us, event | category | flops | bytes accessed | tf_op | source)
XLA Modules:
  0.0 254.0 jit_solution(4007755741568190682)
XLA Ops:
  0.0 1.3 pad.11.first_ref
  1.3 1.3 pad.12.second_ref
  2.6 1.3 pad.13.third_ref
  3.9 1.5 copy.8.of_ref
  5.3 245.6 %shard_map.73 = f32[2,2,128,8,128]{4,3,2,1,0:T(8,128)} custom-call(f32[2,2,128,8,128]{4,3,2,1,0:T(8,128)} %spec_ref.1, f32[2,32,256,64]{3,2,1,0:T(8,128)} %bitcast.4, f32[64,128]{1,0:T(8,128)} %bitcast.5, f32[128,64]{1,0:T(8,128)} %copy.8.of_ref, f32[8,128]{1,0:T(8,128)} %pad.11.first_ref, f32[8,128]{1,0:T(8,128)} %pad.12.second_ref, f32[16,128]{1,0:T(8,128)} %pad.13.third_ref), custom_call_target="tpu_custom_call" | custom-call | tf_op jit(solution)/shard_map/pallas_call | solution.py:354
  250.9 3.0 %copy.10 = f32[2,2,128,8,128]{4,3,2,1,0:T(8,128)} copy(f32[2,2,128,8,128]{4,3,2,1,0:T(8,128)} %shard_map.73) | data formatting | bytes 4194304
where the time goes:
time: 254 us
  Pallas kernels  246 us (97%)
  local copies, waits for them, and re-layouts  8.39 us (3%)
    pallas_call x1, Pallas kernels, per_device(): pl.pallas_call(functools.partial(kernel, (nx, ny, nc, chunks, pc, group,...  246 us

commit v1 on v0

v1 whole, which is shorter than its diff:
```python
import functools

import jax
import jax.numpy as jnp
from jax import lax
from jax.experimental import pallas as pl
from jax.experimental.pallas import tpu as pltpu
from jax.sharding import PartitionSpec as P

MESH = pl.DeviceIdType.MESH
F32 = jnp.float32
BF16 = jnp.bfloat16


def halves(value):
    high = value.astype(BF16)
    return high, (value - high.astype(F32)).astype(BF16)


def whole_div(x, n):
    assert n & (n - 1) == 0
    return x >> (n.bit_length() - 1)


def whole_rem(x, n):
    assert n & (n - 1) == 0
    return x & (n - 1)


def iota(shape, dim):
    return lax.broadcasted_iota(jnp.int32, shape, dim)


def picks_rows(count, width, pick):
    return (pick(iota((count, width), 0)) == iota((count, width), 1)).astype(F32)


def picks_columns(width, count, pick):
    return (iota((width, count), 0) == pick(iota((width, count), 1))).astype(F32)


exact = functools.partial(
    lax.dot_general, precision=lax.Precision.HIGHEST, preferred_element_type=F32
)
plain = functools.partial(lax.dot_general, preferred_element_type=F32)
PLAIN = (((1,), (0,)), ((), ()))
TURNED = (((1,), (1,)), ((), ()))


def dot_split(left, right, how=PLAIN):
    (lh, ll), (rh, rl) = left, right
    return plain(lh, rh, how) + (plain(lh, rl, how) + plain(ll, rh, how))


def dot_stacked(left, right):
    (lh, ll), (rh, rl) = left, right
    n, m = lh.shape[0], rh.shape[1]
    got = plain(
        jnp.concatenate([lh, ll], axis=0), jnp.concatenate([rh, rl], axis=1), PLAIN
    )
    return got[:n, :m] + (got[:n, m:] + got[n:, :m])


def kernel(
    dims,
    spec_ref, core_hbm, ift_ref, oft_ref, first_ref, second_ref, third_ref,
    out_ref,
    core_v, XS, XA, E, C, Y, RX, ZR, FIN, F1, F2, xw, km, ob, fp,
    core_sem, fsend, frecv, hsend, hrecv,
    xsend, xrecv, usend, dsend, zxrecv, esend, erecv, ysend, yrecv, zsend, zrecv,
    wave_sem,
):
    nx, ny, nc, waves, chunks, mc, gang, b_loc, cin, kx_loc, r4, r5 = dims
    mx, my, col = lax.axis_index("mx"), lax.axis_index("my"), lax.axis_index("col")
    lanes = spec_ref.shape[1]
    _, p_loc, tu, q_all = core_hbm.shape
    p_all = ift_ref.shape[0]
    cout = oft_ref.shape[1]
    ky_loc = second_ref.shape[0]
    modes_third = third_ref.shape[0]
    xl = XS.shape[1]
    pair = 2 * p_loc
    wide = 2 * q_all
    rows_b = b_loc * kx_loc
    piece = mc * kx_loc

    def each(low, high, act):
        def step(d, _):
            act(d)
            return 0

        lax.fori_loop(low, high, step, 0)

    def send(src, dst, send_sem, recv_sem, a, b, c):
        return pltpu.make_async_remote_copy(
            src_ref=src, dst_ref=dst, send_sem=send_sem, recv_sem=recv_sem,
            device_id=(a, b, c), device_id_type=MESH,
        )

    def aligned(start, size):
        return pl.ds(pl.multiple_of(start, 8), size)

    core_copy = pltpu.make_async_copy(core_hbm, core_v, core_sem)
    core_copy.start()

    barrier = pltpu.get_barrier_semaphore()

    def tell(sem, a, b, c):
        pl.semaphore_signal(sem, inc=1, device_id=(a, b, c), device_id_type=MESH)

    each(1, nx, lambda d: tell(barrier, lax.rem(mx + d, nx), my, col))
    each(1, ny, lambda d: tell(barrier, mx, lax.rem(my + d, ny), col))
    each(1, nc, lambda d: tell(barrier, mx, my, lax.rem(col + d, nc)))

    def first_copy(d):
        return send(first_ref, F1.at[mx], fsend.at[d], frecv.at[d], lax.rem(mx + d, nx), my, col)

    def first_arrival(d):
        a = lax.rem(mx + nx - d, nx)
        return send(first_ref, F1.at[a], fsend.at[d], frecv.at[d], a, my, col)

    def second_copy(d):
        return send(second_ref, F2.at[my], hsend.at[d], hrecv.at[d], mx, lax.rem(my + d, ny), col)

    def second_arrival(d):
        b = lax.rem(my + ny - d, ny)
        return send(second_ref, F2.at[b], hsend.at[d], hrecv.at[d], mx, b, col)

    def xs_rows(w, j, c):
        return aligned((c * lanes + (w * chunks + j) * mc) * kx_loc, piece)

    def x_copy(w, j, d):
        c = lax.rem(col + d, nc)
        return send(XS.at[xs_rows(w, j, c)], XA.at[mx, j, col], xsend.at[j, d], xrecv.at[j, d], mx, my, c)

    def x_arrival(w, j, d):
        c = lax.rem(col + nc - d, nc)
        return send(XS.at[xs_rows(w, j, c)], XA.at[mx, j, c], xsend.at[j, d], xrecv.at[j, d], mx, my, c)

    def x_up(j, g):
        return send(XA.at[g, j], XA.at[g, j], usend.at[j, g], zxrecv.at[j, g], mx + 1, my, col)

    def x_down(j, g):
        return send(XA.at[g, j], XA.at[g, j], dsend.at[j, g], zxrecv.at[j, g], mx - 1, my, col)

    def c_rows(j, s):
        return aligned((j * ny + s) * (p_loc * mc), p_loc * mc)

    def e_copy(j, d):
        b = lax.rem(my + d, ny)
        return send(E.at[j, b], C.at[c_rows(j, my)], esend.at[j, d], erecv.at[j, d], mx, b, col)

    def e_arrival(j, d):
        b = lax.rem(my + ny - d, ny)
        return send(E.at[j, my], C.at[c_rows(j, b)], esend.at[j, d], erecv.at[j, d], mx, b, col)

    def y_row(j, c, g):
        return ((j * nc + c) * nx + g) * (mc * rows_b)

    def y_copy(j, d):
        c = lax.rem(col + d, nc)
        return send(
            Y.at[aligned(y_row(j, c, 0), nx * mc * rows_b)], RX.at[j, d - 1],
            ysend.at[j, d], yrecv.at[j, d], mx, my, c,
        )

    def y_arrival(j, d):
        c = lax.rem(col + nc - d, nc)
        return send(
            Y.at[aligned(y_row(j, c, 0), nx * mc * rows_b)], RX.at[j, d - 1],
            ysend.at[j, d], yrecv.at[j, d], mx, my, c,
        )

    def z_move(j, g, slot, a):
        return send(
            Y.at[aligned(y_row(j, col, g), mc * rows_b)], ZR.at[j, slot],
            zsend.at[j, g], zrecv.at[j, slot], a, my, col,
        )

    n, m = 2 * b_loc * cin, nc * xl
    base = exact(
        ift_ref[...].T,
        picks_columns(
            p_all, m,
            lambda j: whole_div(j, xl) * p_loc + whole_rem(j, p_loc),
        ),
        PLAIN,
    )
    base = jnp.concatenate([base] * (2 * b_loc), axis=0)
    row, column = iota((n, m), 0), whole_rem(iota((n, m), 1), xl)
    part, sample = whole_div(row, b_loc * cin), whole_rem(whole_div(row, cin), b_loc)
    same = whole_div(column, p_loc) == sample * 2 + part
    xw[0], xw[1] = halves(jnp.where(same, base, 0.0))

    def rank(k, _):
        block = spec_ref[pl.ds(k, n, stride=kx_loc), :].T
        got = dot_split(halves(block), (xw[0], xw[1]))
        for c in range(nc):
            XS[pl.ds(c * lanes * kx_loc + k, lanes, stride=kx_loc), :] = got[:, c * xl : (c + 1) * xl]
        return 0

    pl.semaphore_wait(barrier, nx - 1 + ny - 1 + nc - 1)
    each(1, nx, lambda d: first_copy(d).start())
    each(1, ny, lambda d: second_copy(d).start())
    F1[mx] = first_ref[...]
    F2[my] = second_ref[...]
    lax.fori_loop(0, kx_loc, rank, 0)

    oft = oft_ref[...].T
    none = jnp.zeros_like(oft)
    ob[0], ob[1] = halves(
        jnp.concatenate(
            [jnp.concatenate([oft, none], axis=1), jnp.concatenate([none, oft], axis=1)], axis=0
        )
    )

    def start_spectrum(w):
        def go(j, _):
            each(1, nc, lambda d: x_copy(w, j, d).start())
            XA[mx, j, col] = XS[xs_rows(w, j, col), :]
            return 0

        lax.fori_loop(0, chunks, go, 0)

    start_spectrum(0)

    each(1, nx, lambda d: first_arrival(d).wait_recv())
    each(1, ny, lambda d: second_arrival(d).wait_recv())
    n, m = ny * lanes, tu

    def mode_of(r):
        return whole_div(r, ny * mc) * mc + whole_rem(r, mc)

    by_second = exact(
        exact(
            picks_rows(
                n, ny * ky_loc,
                lambda r: whole_rem(whole_div(r, mc), ny) * ky_loc + whole_div(mode_of(r), modes_third),
            ),
            F2[...].reshape(ny * ky_loc, r4),
            PLAIN,
        ),
        picks_columns(r4, m, lambda j: whole_div(j, r5)),
        PLAIN,
    )
    by_third = exact(
        exact(
            picks_rows(n, modes_third, lambda r: whole_rem(mode_of(r), modes_third)),
            third_ref[...],
            PLAIN,
        ),
        picks_columns(r5, m, lambda j: whole_rem(j, r5)),
        PLAIN,
    )
    km[0], km[1] = halves(by_second * by_third)
    r3 = F1.shape[2]
    fp[...] = exact(
        exact(
            picks_rows(
                nx * nc * kx_loc, nx * kx_loc,
                lambda r: whole_div(r, nc * kx_loc) * kx_loc + whole_rem(r, kx_loc),
            ),
            F1[...].reshape(nx * kx_loc, r3),
            PLAIN,
        ),
        picks_columns(r3, ny * pair, lambda j: mx * ny + whole_div(j, pair)),
        PLAIN,
    )
    core_copy.wait()

    def expand(w, k):
        rows = gang * ny * mc
        start = pl.multiple_of((w * chunks + k * gang) * ny * mc, rows)
        left = (km[0, pl.ds(start, rows), :], km[1, pl.ds(start, rows), :])

        def one(p, _):
            right = jnp.concatenate([core_v[0, p], core_v[1, p]], axis=1)
            got = dot_stacked(left, halves(right))
            for i in range(gang):
                for b in range(ny):
                    r = (i * ny + b) * mc
                    E[k * gang + i, b, aligned(p * mc, mc), :] = got[r : r + mc]
            return 0

        lax.fori_loop(0, p_loc, one, 0)

        def go(i, _):
            j = k * gang + i
            each(1, ny, lambda d: e_copy(j, d).start())
            C[c_rows(j, my), :] = E[j, my]
            return 0

        lax.fori_loop(0, gang, go, 0)

    sign = jnp.where(iota((p_loc, wide), 1) < q_all, -1.0, 1.0).astype(F32)

    def contract(j):
        def one(i, _):
            here = XA[:, j, :, aligned(i * kx_loc, kx_loc), :].reshape(nx * nc * kx_loc, xl)
            lefts = []
            for b in range(b_loc):
                block = here[:, b * pair : (b + 1) * pair]
                lefts.append(jnp.concatenate([block] * ny, axis=1) * fp[...])
            rights = []
            for s in range(ny):
                block = C[pl.ds((j * ny + s) * (p_loc * mc) + i, p_loc, stride=mc), :]
                rights += [block, pltpu.roll(block, q_all, 1) * sign]
            got = dot_stacked(
                halves(jnp.concatenate(lefts, axis=0)), halves(jnp.concatenate(rights, axis=0))
            )
            for b in range(b_loc):
                for g in range(nx):
                    for c in range(nc):
                        r = ((b * nx + g) * nc + c) * kx_loc
                        Y[aligned(y_row(j, c, g) + i * rows_b + b * kx_loc, kx_loc), :] = got[r : r + kx_loc]
            return 0

        lax.fori_loop(0, mc, one, 0, unroll=2)

    def wave(w):
        def tick(step, _):
            t = step - (nx - 1)

            @pl.when(step < chunks // gang)
            def _():
                expand(w, step)

            @pl.when(step < chunks)
            def _():
                each(1, nc, lambda d: x_arrival(w, step, d).wait_recv())

                @pl.when(mx < nx - 1)
                def _():
                    x_up(step, mx).start()

                @pl.when(mx > 0)
                def _():
                    x_down(step, mx).start()

            for h in range(1, nx):
                j = step - h

                @pl.when((j >= 0) & (j < chunks))
                def _():
                    @pl.when(mx >= h)
                    def _():
                        x_up(j, mx - h).wait_recv()

                        @pl.when(mx < nx - 1)
                        def _():
                            x_up(j, mx - h).start()

                    @pl.when(mx + h < nx)
                    def _():
                        x_down(j, mx + h).wait_recv()

                        @pl.when(mx > 0)
                        def _():
                            x_down(j, mx + h).start()

            @pl.when((t >= 0) & (t < chunks))
            def _():
                each(1, ny, lambda d: e_arrival(t, d).wait_recv())
                contract(t)
                each(1, nc, lambda d: y_copy(t, d).start())

            j = t - 1

            @pl.when((j >= 0) & (j < chunks))
            def _():
                each(1, nc, lambda d: y_arrival(j, d).wait_recv())
                size = mc * rows_b

                def add(g, _):
                    rows = aligned(y_row(j, col, g), size)
                    total = Y[rows, :]
                    for d in range(1, nc):
                        total = total + RX[j, d - 1, aligned(g * size, size), :]
                    Y[rows, :] = total
                    return 0

                lax.fori_loop(0, nx, add, 0)

            up = t - 1 - mx

            @pl.when((up >= 0) & (up < chunks))
            def _():
                for g in range(nx):
                    @pl.when((mx > 0) & (g >= mx))
                    def _():
                        slot = jnp.where(g == mx, nx, g)
                        z_move(up, g, slot, mx - 1).wait_recv()
                        Y[aligned(y_row(up, col, g), mc * rows_b), :] += ZR[up, slot]

                    @pl.when(g > mx)
                    def _():
                        z_move(up, g, jnp.where(g == mx + 1, nx, g), mx + 1).start()

            down = t - 1 - (nx - 1 - mx)

            @pl.when((down >= 0) & (down < chunks))
            def _():
                for g in range(nx):
                    @pl.when((mx < nx - 1) & (g <= mx))
                    def _():
                        z_move(down, g, g, mx + 1).wait_recv()
                        Y[aligned(y_row(down, col, g), mc * rows_b), :] += ZR[down, g]

                    @pl.when(g < mx)
                    def _():
                        z_move(down, g, g, mx - 1).start()

            done = t - 1 - jnp.maximum(mx, nx - 1 - mx)

            @pl.when((done >= 0) & (done < chunks))
            def _():
                for r in range(rows_b):
                    FIN[r, aligned((w * chunks + done) * mc, mc), :] = Y[
                        pl.ds(y_row(done, col, mx) + r, mc, stride=rows_b), :
                    ]

            return 0

        lax.fori_loop(0, chunks + 2 * nx - 1, tick, 0)

        def finish(j, _):
            each(1, nc, lambda d: x_copy(w, j, d).wait_send())
            each(1, ny, lambda d: e_copy(j, d).wait_send())
            each(1, nc, lambda d: y_copy(j, d).wait_send())
            for g in range(nx):
                @pl.when((g <= mx) & (mx < nx - 1))
                def _():
                    x_up(j, g).wait_send()

                @pl.when((g >= mx) & (mx > 0))
                def _():
                    x_down(j, g).wait_send()

                @pl.when(g > mx)
                def _():
                    z_move(j, g, g, mx + 1).wait_send()

                @pl.when(g < mx)
                def _():
                    z_move(j, g, g, mx - 1).wait_send()

            return 0

        lax.fori_loop(0, chunks, finish, 0)

    wave(0)
    if waves > 1:
        def again(w, _):
            @pl.when(mx < nx - 1)
            def _():
                tell(wave_sem, mx + 1, my, col)

            @pl.when(mx > 0)
            def _():
                tell(wave_sem, mx - 1, my, col)

            each(1, ny, lambda d: tell(wave_sem, mx, lax.rem(my + d, ny), col))
            each(1, nc, lambda d: tell(wave_sem, mx, my, lax.rem(col + d, nc)))
            near = (mx < nx - 1).astype(jnp.int32) + (mx > 0).astype(jnp.int32)
            pl.semaphore_wait(wave_sem, near + ny - 1 + nc - 1)
            start_spectrum(w)
            wave(w)
            return 0

        lax.fori_loop(1, waves, again, 0)

    def result(r, _):
        b, k = whole_div(r, kx_loc), whole_rem(r, kx_loc)
        got = dot_split((ob[0], ob[1]), halves(FIN[r]), TURNED)
        for c in range(2):
            out_ref[pl.ds((c * b_loc + b) * cout * kx_loc + k, cout, stride=kx_loc), :] = got[
                c * cout : (c + 1) * cout
            ]
        return 0

    lax.fori_loop(0, rows_b, result, 0)
    each(1, nx, lambda d: first_copy(d).wait_send())
    each(1, ny, lambda d: second_copy(d).wait_send())


def per_device(
    nx, ny, nc,
    spectrum, core_tensor, input_factor, output_factor, first_factor, second_factor, third_factor,
):
    _, b_loc, cin, kx_loc, lanes = spectrum.shape
    _, p_loc, q_all, _, r4, r5 = core_tensor.shape
    cout = output_factor.shape[0]
    r3 = first_factor.shape[1]
    ky_loc = second_factor.shape[0]
    assert r3 == nx * ny
    tu = r4 * r5
    mc = 8
    xl = -(-(b_loc * 2 * p_loc) // 128) * 128
    rows_b = b_loc * kx_loc
    wide = 2 * q_all

    def buffers(chunks):
        return [
            (2, p_loc, tu, q_all),
            (nc * lanes * kx_loc, xl),
            (nx, chunks, nc, mc * kx_loc, xl),
            (chunks, ny, p_loc * mc, wide),
            (chunks * ny * p_loc * mc, wide),
            (chunks * nc * nx * mc * rows_b, wide),
            (chunks, max(nc - 1, 1), nx * mc * rows_b, wide),
            (chunks, nx + 1, mc * rows_b, wide),
            (rows_b, lanes, wide),
        ]

    def held(shape):
        size = 4 * -(-shape[-1] // 128) * 128
        for extent in shape[:-1]:
            size *= extent
        return size

    waves = 1
    fixed = 2 * 4 * lanes * 2 * b_loc * kx_loc * max(cin, cout)
    while fixed + sum(map(held, buffers(lanes // mc // waves))) > 56 * 2**20:
        waves *= 2
    chunks = lanes // mc // waves
    gang = min(chunks, max(1, 128 // (ny * mc)))

    core = jnp.transpose(core_tensor, (0, 1, 3, 4, 5, 2)).reshape(2, p_loc, tu, q_all)
    vmem = pl.BlockSpec(memory_space=pltpu.VMEM)
    dma = pltpu.SemaphoreType.DMA
    out = pl.pallas_call(
        functools.partial(
            kernel, (nx, ny, nc, waves, chunks, mc, gang, b_loc, cin, kx_loc, r4, r5)
        ),
        out_shape=jax.ShapeDtypeStruct((2 * b_loc * cout * kx_loc, lanes), F32),
        in_specs=[vmem, pl.BlockSpec(memory_space=pl.ANY)] + [vmem] * 5,
        out_specs=vmem,
        scratch_shapes=[pltpu.VMEM(shape, F32) for shape in buffers(chunks)]
        + [
            pltpu.VMEM((nx, kx_loc, r3), F32),
            pltpu.VMEM((ny, ky_loc, r4), F32),
            pltpu.VMEM((2, 2 * b_loc * cin, nc * xl), BF16),
            pltpu.VMEM((2, ny * lanes, tu), BF16),
            pltpu.VMEM((2, 2 * cout, wide), BF16),
            pltpu.VMEM((nx * nc * kx_loc, ny * 2 * p_loc), F32),
            dma,
            dma((nx,)), dma((nx,)), dma((ny,)), dma((ny,)),
            dma((chunks, nc)), dma((chunks, nc)),
            dma((chunks, nx)), dma((chunks, nx)), dma((chunks, nx)),
            dma((chunks, ny)), dma((chunks, ny)),
            dma((chunks, nc)), dma((chunks, nc)),
            dma((chunks, nx)), dma((chunks, nx + 1)),
            pltpu.SemaphoreType.REGULAR,
        ],
        compiler_params=pltpu.CompilerParams(
            collective_id=0, has_side_effects=True, vmem_limit_bytes=61000 * 1024
        ),
    )(
        spectrum.reshape(2 * b_loc * cin * kx_loc, lanes), core,
        input_factor.T, output_factor.T, first_factor, second_factor, third_factor,
    )
    return out.reshape(2, b_loc, cout, kx_loc, lanes)


def solution(mesh):
    placed = (
        P(None, "col", None, "mx", "my"),
        P(None, "col", None, ("mx", "my"), None, None),
        P(),
        P(),
        P("mx", None),
        P("my", None),
        P(),
    )
    return jax.shard_map(
        functools.partial(
            per_device, mesh.shape["mx"], mesh.shape["my"], mesh.shape["col"]
        ),
        mesh=mesh,
        in_specs=placed,
        out_specs=P(None, "col", None, "mx", "my"),
        check_vma=False,
    )
```

time: 254 us -> 168 us (0.66)
  the two profiles are of different devices: /device:TPU:28 before, /device:TPU:0 now
where the time goes in v1:
time: 168 us; the launch traced here: 166 us
  Pallas kernels  163 us (97%)
  local copies, waits for them, and re-layouts  3.05 us (2%)
    pallas_call x1, Pallas kernels, per_device(): pl.pallas_call(functools.partial(kernel, (nx, ny, nc, waves, chunks, mc,...  163 us

profile of v1, /device:TPU:0, one launch (start us, length us, event | category | flops | bytes accessed | tf_op | source)
XLA Modules:
  0.0 166.0 jit_solution(13591445026713134914)
XLA Ops:
  0.0 163.0 %shard_map.73 = f32[4096,128]{1,0:T(8,128)} custom-call(f32[4096,128]{1,0:T(8,128)} %bitcast.9, f32[2,32,256,64]{3,2,1,0:T(8,128)} %bitcast.7, f32[64,128]{1,0:T(8,128)} %bitcast.10, f32[64,128]{1,0:T(8,128)} %bitcast.11, f32[8,16]{1,0:T(8,128)} %first_ref.1, f32[8,16]{1,0:T(8,128)} %second_ref.1, f32[16,16]{1,0:T(8,128)} %third_ref.1), custom_call_target="tpu_custom_call" | custom-call | tf_op jit(solution)/shard_map/pallas_call | solution.py:531
  163.0 3.0 %copy.9 = f32[2,2,128,8,128]{4,3,2,1,0:T(8,128)} copy(f32[2,2,128,8,128]{4,3,2,1,0:T(8,128)} %bitcast.8) | data formatting | bytes 4194304

commit v2 on v1

v2 whole, which is shorter than its diff:
```python
import functools

import jax
import jax.numpy as jnp
from jax import lax
from jax.experimental import pallas as pl
from jax.experimental.pallas import tpu as pltpu
from jax.sharding import PartitionSpec as P

MESH = pl.DeviceIdType.MESH
F32 = jnp.float32
BF16 = jnp.bfloat16


def halves(value):
    high = value.astype(BF16)
    return high, (value - high.astype(F32)).astype(BF16)


def whole_div(x, n):
    assert n & (n - 1) == 0
    return x >> (n.bit_length() - 1)


def whole_rem(x, n):
    assert n & (n - 1) == 0
    return x & (n - 1)


def iota(shape, dim):
    return lax.broadcasted_iota(jnp.int32, shape, dim)


def picks_rows(count, width, pick):
    return (pick(iota((count, width), 0)) == iota((count, width), 1)).astype(F32)


def picks_columns(width, count, pick):
    return (iota((width, count), 0) == pick(iota((width, count), 1))).astype(F32)


exact = functools.partial(
    lax.dot_general, precision=lax.Precision.HIGHEST, preferred_element_type=F32
)
plain = functools.partial(lax.dot_general, preferred_element_type=F32)
PLAIN = (((1,), (0,)), ((), ()))
TURNED = (((1,), (1,)), ((), ()))


def dot_split(left, right, how=PLAIN):
    (lh, ll), (rh, rl) = left, right
    return plain(lh, rh, how) + (plain(lh, rl, how) + plain(ll, rh, how))


def dot_stacked(left, right):
    (lh, ll), (rh, rl) = left, right
    n, m = lh.shape[0], rh.shape[1]
    got = plain(
        jnp.concatenate([lh, ll], axis=0), jnp.concatenate([rh, rl], axis=1), PLAIN
    )
    return got[:n, :m] + (got[:n, m:] + got[n:, :m])


def kernel(
    dims,
    spec_ref, core_hbm, ift_ref, first_ref, second_ref, third_ref,
    FIN,
    core_v, XS, XA, E, C, Y, RX, ZR, F1, F2, xw, km, ready, fp,
    core_sem, fsend, frecv, hsend, hrecv,
    xsend, xrecv, usend, dsend, zxrecv, esend, erecv, ysend, yrecv, zsend, zrecv,
    fin_sem, wave_sem,
):
    nx, ny, nc, waves, chunks, mc, gang, sub, lag, hop, b_loc, cin, kx_loc, r4, r5 = dims
    mx, my, col = lax.axis_index("mx"), lax.axis_index("my"), lax.axis_index("col")
    lanes = spec_ref.shape[1]
    _, p_loc, tu, q_all = core_hbm.shape
    p_all = ift_ref.shape[0]
    ky_loc = second_ref.shape[0]
    modes_third = third_ref.shape[0]
    xl = XS.shape[1]
    pair = 2 * p_loc
    wide = 2 * q_all
    rows_b = b_loc * kx_loc
    my_modes = mc // sub
    piece = mc * kx_loc

    def each(low, high, act):
        def step(d, _):
            act(d)
            return 0

        lax.fori_loop(low, high, step, 0)

    def send(src, dst, send_sem, recv_sem, a, b, c):
        return pltpu.make_async_remote_copy(
            src_ref=src, dst_ref=dst, send_sem=send_sem, recv_sem=recv_sem,
            device_id=(a, b, c), device_id_type=MESH,
        )

    def aligned(start, size):
        return pl.ds(pl.multiple_of(start, 8), size)

    core_copy = pltpu.make_async_copy(core_hbm, core_v, core_sem)
    core_copy.start()

    barrier = pltpu.get_barrier_semaphore()

    def tell(sem, a, b, c):
        pl.semaphore_signal(sem, inc=1, device_id=(a, b, c), device_id_type=MESH)

    each(1, nx, lambda d: tell(barrier, lax.rem(mx + d, nx), my, col))
    each(1, ny, lambda d: tell(barrier, mx, lax.rem(my + d, ny), col))
    each(1, nc, lambda d: tell(barrier, mx, my, lax.rem(col + d, nc)))

    def first_copy(d):
        return send(first_ref, F1.at[mx], fsend.at[d], frecv.at[d], lax.rem(mx + d, nx), my, col)

    def first_arrival(d):
        a = lax.rem(mx + nx - d, nx)
        return send(first_ref, F1.at[a], fsend.at[d], frecv.at[d], a, my, col)

    def second_copy(d):
        return send(second_ref, F2.at[my], hsend.at[d], hrecv.at[d], mx, lax.rem(my + d, ny), col)

    def second_arrival(d):
        b = lax.rem(my + ny - d, ny)
        return send(second_ref, F2.at[b], hsend.at[d], hrecv.at[d], mx, b, col)

    def xs_rows(w, j, c):
        return aligned((c * lanes + (w * chunks + j) * mc) * kx_loc, piece)

    def x_copy(w, j, d):
        c = lax.rem(col + d, nc)
        return send(XS.at[xs_rows(w, j, c)], XA.at[mx, j, col], xsend.at[j, d], xrecv.at[j, d], mx, my, c)

    def x_arrival(w, j, d):
        c = lax.rem(col + nc - d, nc)
        return send(XS.at[xs_rows(w, j, c)], XA.at[mx, j, c], xsend.at[j, d], xrecv.at[j, d], mx, my, c)

    def x_up(j, g):
        return send(XA.at[g, j], XA.at[g, j], usend.at[j, g], zxrecv.at[j, g], mx + 1, my, col)

    def x_down(j, g):
        return send(XA.at[g, j], XA.at[g, j], dsend.at[j, g], zxrecv.at[j, g], mx - 1, my, col)

    def c_rows(j, s):
        return aligned((j * ny + s) * (p_loc * mc), p_loc * mc)

    def e_copy(j, d):
        b = lax.rem(my + d, ny)
        return send(E.at[j, b], C.at[c_rows(j, my)], esend.at[j, d], erecv.at[j, d], mx, b, col)

    def e_arrival(j, d):
        b = lax.rem(my + ny - d, ny)
        return send(E.at[j, my], C.at[c_rows(j, b)], esend.at[j, d], erecv.at[j, d], mx, b, col)

    def y_row(j, c, g):
        return ((j * nc + c) * nx + g) * (my_modes * rows_b)

    def y_copy(j, d):
        c = lax.rem(col + d, nc)
        return send(
            Y.at[aligned(y_row(j, c, 0), nx * my_modes * rows_b)], RX.at[j, d - 1],
            ysend.at[j, d], yrecv.at[j, d], mx, my, c,
        )

    def y_arrival(j, d):
        c = lax.rem(col + nc - d, nc)
        return send(
            Y.at[aligned(y_row(j, c, 0), nx * my_modes * rows_b)], RX.at[j, d - 1],
            ysend.at[j, d], yrecv.at[j, d], mx, my, c,
        )

    def z_move(j, g, slot, a):
        return send(
            Y.at[aligned(y_row(j, col, g), my_modes * rows_b)], ZR.at[j, slot],
            zsend.at[j, g], zrecv.at[j, slot], a, my, col,
        )

    def fin_copy(w, t):
        rows = my_modes * rows_b
        return pltpu.make_async_copy(
            Y.at[aligned(y_row(t, col, mx), rows)],
            FIN.at[aligned((w * chunks * sub + t) * rows, rows)],
            fin_sem.at[t],
        )

    n, m = 2 * b_loc * cin, nc * xl
    base = exact(
        ift_ref[...].T,
        picks_columns(
            p_all, m,
            lambda j: whole_div(j, xl) * p_loc + whole_rem(j, p_loc),
        ),
        PLAIN,
    )
    base = jnp.concatenate([base] * (2 * b_loc), axis=0)
    row, column = iota((n, m), 0), whole_rem(iota((n, m), 1), xl)
    part, sample = whole_div(row, b_loc * cin), whole_rem(whole_div(row, cin), b_loc)
    same = whole_div(column, p_loc) == sample * 2 + part
    xw[0], xw[1] = halves(jnp.where(same, base, 0.0))

    def rank(k, _):
        block = spec_ref[pl.ds(k, n, stride=kx_loc), :].T
        got = dot_split(halves(block), (xw[0], xw[1]))
        for c in range(nc):
            XS[pl.ds(c * lanes * kx_loc + k, lanes, stride=kx_loc), :] = got[:, c * xl : (c + 1) * xl]
        return 0

    lax.fori_loop(0, kx_loc, rank, 0)
    by_third = exact(third_ref[...], picks_columns(r5, tu, lambda j: whole_rem(j, r5)), PLAIN)

    def start_spectrum(w):
        def go(j, _):
            each(1, nc, lambda d: x_copy(w, j, d).start())
            XA[mx, j, col] = XS[xs_rows(w, j, col), :]
            return 0

        lax.fori_loop(0, chunks, go, 0)

    F1[mx] = first_ref[...]
    F2[my] = second_ref[...]
    pl.semaphore_wait(barrier, nx - 1 + ny - 1 + nc - 1)
    each(1, ny, lambda d: second_copy(d).start())
    each(1, nx, lambda d: first_copy(d).start())
    start_spectrum(0)
    core_copy.wait()

    def prepare(p, _):
        ready[p, :, :wide], ready[p, :, wide:] = halves(
            jnp.concatenate([core_v[0, p], core_v[1, p]], axis=1)
        )
        return 0

    lax.fori_loop(0, p_loc, prepare, 0, unroll=2)
    each(1, ny, lambda d: second_arrival(d).wait_recv())
    by_second = exact(
        F2[...].reshape(ny * ky_loc, r4),
        picks_columns(r4, tu, lambda j: whole_div(j, r5)),
        PLAIN,
    )
    assert modes_third % mc == 0 and ny % 2 == 0
    for j in range(lanes // mc):
        k = j * mc % modes_third
        for b in range(0, ny, 2):
            r = [(b + i) * ky_loc + j * mc // modes_third for i in range(2)]
            tile = jnp.concatenate(
                [by_second[i : i + 1, :] * by_third[k : k + mc, :] for i in r], axis=0
            )
            km[0, (j * ny + b) * mc : (j * ny + b + 2) * mc, :], km[1, (j * ny + b) * mc : (j * ny + b + 2) * mc, :] = halves(tile)

    def expand(w, k):
        rows = gang * ny * mc
        start = pl.multiple_of((w * chunks + k * gang) * ny * mc, rows)
        left = jnp.concatenate([km[0, pl.ds(start, rows), :], km[1, pl.ds(start, rows), :]], axis=0)

        def one(p, _):
            got = plain(left, ready[p], PLAIN)
            got = got[:rows, :wide] + (got[:rows, wide:] + got[rows:, :wide])
            for i in range(gang):
                for b in range(ny):
                    r = (i * ny + b) * mc
                    E[k * gang + i, b, aligned(p * mc, mc), :] = got[r : r + mc]
            return 0

        lax.fori_loop(0, p_loc, one, 0, unroll=4)

        def go(i, _):
            j = k * gang + i
            each(1, ny, lambda d: e_copy(j, d).start())
            C[c_rows(j, my), :] = E[j, my]
            return 0

        lax.fori_loop(0, gang, go, 0)

    sign = jnp.where(iota((p_loc, wide), 1) < q_all, -1.0, 1.0).astype(F32)

    def spread_first():
        each(1, nx, lambda d: first_arrival(d).wait_recv())
        r3 = F1.shape[2]
        fp[...] = exact(
            exact(
                picks_rows(
                    nx * nc * kx_loc, nx * kx_loc,
                    lambda r: whole_div(r, nc * kx_loc) * kx_loc + whole_rem(r, kx_loc),
                ),
                F1[...].reshape(nx * kx_loc, r3),
                PLAIN,
            ),
            picks_columns(r3, ny * pair, lambda j: mx * ny + whole_div(j, pair)),
            PLAIN,
        )

    def contract(t):
        j, first = whole_div(t, sub), whole_rem(t, sub) * my_modes

        def one(i, _):
            k = first + i
            here = XA[:, j, :, aligned(k * kx_loc, kx_loc), :].reshape(nx * nc * kx_loc, xl)
            lefts = []
            for b in range(b_loc):
                block = here[:, b * pair : (b + 1) * pair]
                lefts.append(jnp.concatenate([block] * ny, axis=1) * fp[...])
            rights = []
            for s in range(ny):
                block = C[pl.ds((j * ny + s) * (p_loc * mc) + k, p_loc, stride=mc), :]
                rights += [block, pltpu.roll(block, q_all, 1) * sign]
            got = dot_stacked(
                halves(jnp.concatenate(lefts, axis=0)), halves(jnp.concatenate(rights, axis=0))
            )
            for b in range(b_loc):
                for g in range(nx):
                    for c in range(nc):
                        r = ((b * nx + g) * nc + c) * kx_loc
                        Y[aligned(y_row(t, c, g) + i * rows_b + b * kx_loc, kx_loc), :] = got[r : r + kx_loc]
            return 0

        lax.fori_loop(0, my_modes, one, 0, unroll=2)

    def spectrum_out(w, j):
        @pl.when(j < chunks)
        def _():
            each(1, nc, lambda d: x_arrival(w, j, d).wait_recv())

            @pl.when(mx < nx - 1)
            def _():
                x_up(j, mx).start()

            @pl.when(mx > 0)
            def _():
                x_down(j, mx).start()

    def spectrum_on(j, h):
        @pl.when(j < chunks)
        def _():
            @pl.when(mx >= h)
            def _():
                x_up(j, mx - h).wait_recv()

                @pl.when(mx < nx - 1)
                def _():
                    x_up(j, mx - h).start()

            @pl.when(mx + h < nx)
            def _():
                x_down(j, mx + h).wait_recv()

                @pl.when(mx > 0)
                def _():
                    x_down(j, mx + h).start()

    def expand_if(w, k):
        @pl.when(k < chunks // gang)
        def _():
            expand(w, k)

    def lead(w):
        for step in range(nx - 1):
            spectrum_out(w, step)
            for h in range(1, step + 1):
                spectrum_on(step - h, h)
            if step < nx - 2:
                expand_if(w, step)
            if step == 0 and isinstance(w, int):
                spread_first()

    def wave(w):
        total = chunks * sub

        def later(t):
            j = t - lag

            @pl.when((j >= 0) & (j < total))
            def _():
                each(1, nc, lambda d: y_arrival(j, d).wait_recv())
                size = my_modes * rows_b

                def add(g, _):
                    rows = aligned(y_row(j, col, g), size)
                    own = Y[rows, :]
                    for d in range(1, nc):
                        own = own + RX[j, d - 1, aligned(g * size, size), :]
                    Y[rows, :] = own
                    return 0

                lax.fori_loop(0, nx, add, 0)

            up = t - lag - hop * mx

            @pl.when((up >= 0) & (up < total))
            def _():
                for g in range(nx - 1, -1, -1):
                    @pl.when((mx > 0) & (g >= mx))
                    def _():
                        slot = jnp.where(g == mx, nx, g)
                        z_move(up, g, slot, mx - 1).wait_recv()
                        Y[aligned(y_row(up, col, g), my_modes * rows_b), :] += ZR[up, slot]

                    @pl.when(g > mx)
                    def _():
                        z_move(up, g, jnp.where(g == mx + 1, nx, g), mx + 1).start()

            down = t - lag - hop * (nx - 1 - mx)

            @pl.when((down >= 0) & (down < total))
            def _():
                for g in range(nx):
                    @pl.when((mx < nx - 1) & (g <= mx))
                    def _():
                        z_move(down, g, g, mx + 1).wait_recv()
                        Y[aligned(y_row(down, col, g), my_modes * rows_b), :] += ZR[down, g]

                    @pl.when(g < mx)
                    def _():
                        z_move(down, g, g, mx - 1).start()

            done = t - lag - hop * jnp.maximum(mx, nx - 1 - mx)

            @pl.when((done >= 0) & (done < total))
            def _():
                fin_copy(w, done).start()

        def tick(j, _):
            expand_if(w, j + nx - 2)
            spectrum_out(w, j + nx - 1)
            for h in range(1, nx):
                spectrum_on(j + nx - 1 - h, h)

            @pl.when(j < chunks)
            def _():
                each(1, ny, lambda d: e_arrival(j, d).wait_recv())

            def part(u, _):
                t = j * sub + u

                @pl.when(t < total)
                def _():
                    contract(t)
                    each(1, nc, lambda d: y_copy(t, d).start())

                later(t)
                return 0

            lax.fori_loop(0, sub, part, 0)
            return 0

        lax.fori_loop(0, chunks + -(-(lag + hop * (nx - 1)) // sub), tick, 0)

        def finish(j, _):
            each(1, nc, lambda d: x_copy(w, j, d).wait_send())
            each(1, ny, lambda d: e_copy(j, d).wait_send())
            for g in range(nx):
                @pl.when((g <= mx) & (mx < nx - 1))
                def _():
                    x_up(j, g).wait_send()

                @pl.when((g >= mx) & (mx > 0))
                def _():
                    x_down(j, g).wait_send()

            return 0

        def finish_part(t, _):
            each(1, nc, lambda d: y_copy(t, d).wait_send())
            for g in range(nx):
                @pl.when(g > mx)
                def _():
                    z_move(t, g, g, mx + 1).wait_send()

                @pl.when(g < mx)
                def _():
                    z_move(t, g, g, mx - 1).wait_send()

            fin_copy(w, t).wait()
            return 0

        lax.fori_loop(0, chunks, finish, 0)
        lax.fori_loop(0, total, finish_part, 0)

    lead(0)
    wave(0)
    if waves > 1:
        def again(w, _):
            @pl.when(mx < nx - 1)
            def _():
                tell(wave_sem, mx + 1, my, col)

            @pl.when(mx > 0)
            def _():
                tell(wave_sem, mx - 1, my, col)

            each(1, ny, lambda d: tell(wave_sem, mx, lax.rem(my + d, ny), col))
            each(1, nc, lambda d: tell(wave_sem, mx, my, lax.rem(col + d, nc)))
            near = (mx < nx - 1).astype(jnp.int32) + (mx > 0).astype(jnp.int32)
            pl.semaphore_wait(wave_sem, near + ny - 1 + nc - 1)
            start_spectrum(w)
            lead(w)
            wave(w)
            return 0

        lax.fori_loop(1, waves, again, 0)

    each(1, nx, lambda d: first_copy(d).wait_send())
    each(1, ny, lambda d: second_copy(d).wait_send())


def mix(lanes, oft_ref, fin_ref, out_ref):
    cout = oft_ref.shape[1]
    kx_loc = out_ref.shape[2] // cout
    rows_b = fin_ref.shape[0] // lanes
    first = pl.program_id(0) * kx_loc
    oft = oft_ref[...].T
    none = jnp.zeros_like(oft)
    ob = halves(
        jnp.concatenate(
            [jnp.concatenate([oft, none], axis=1), jnp.concatenate([none, oft], axis=1)], axis=0
        )
    )
    for k in range(kx_loc):
        rows = pl.ds(first + k, lanes, stride=rows_b)
        got = dot_split(ob, halves(fin_ref[rows, :]), TURNED)
        for c in range(2):
            out_ref[c, 0, pl.ds(k, cout, stride=kx_loc), :] = got[c * cout : (c + 1) * cout]


def per_device(
    nx, ny, nc,
    spectrum, core_tensor, input_factor, output_factor, first_factor, second_factor, third_factor,
):
    _, b_loc, cin, kx_loc, lanes = spectrum.shape
    _, p_loc, q_all, _, r4, r5 = core_tensor.shape
    cout = output_factor.shape[0]
    r3 = first_factor.shape[1]
    ky_loc = second_factor.shape[0]
    assert r3 == nx * ny
    tu = r4 * r5
    mc, sub, lag, hop = 8, 2, 2, 3
    xl = -(-(b_loc * 2 * p_loc) // 128) * 128
    rows_b = b_loc * kx_loc
    wide = 2 * q_all

    def buffers(chunks):
        return [
            (2, p_loc, tu, q_all),
            (nc * lanes * kx_loc, xl),
            (nx, chunks, nc, mc * kx_loc, xl),
            (chunks, ny, p_loc * mc, wide),
            (chunks * ny * p_loc * mc, wide),
            (chunks * nc * nx * mc * rows_b, wide),
            (chunks * sub, max(nc - 1, 1), nx * (mc // sub) * rows_b, wide),
            (chunks * sub, nx + 1, mc // sub * rows_b, wide),
        ]

    def held(shape):
        size = 4 * -(-shape[-1] // 128) * 128
        for extent in shape[:-1]:
            size *= extent
        return size

    waves = 1
    fixed = 4 * lanes * rows_b * 2 * cin + 4 * p_loc * tu * wide
    while fixed + sum(map(held, buffers(lanes // mc // waves))) > 58 * 2**20:
        waves *= 2
    chunks = lanes // mc // waves
    gang = min(chunks, max(1, 64 // (ny * mc)))

    core = jnp.transpose(core_tensor, (0, 1, 3, 4, 5, 2)).reshape(2, p_loc, tu, q_all)
    vmem = pl.BlockSpec(memory_space=pltpu.VMEM)
    dma = pltpu.SemaphoreType.DMA
    fin = pl.pallas_call(
        functools.partial(
            kernel, (nx, ny, nc, waves, chunks, mc, gang, sub, lag, hop, b_loc, cin, kx_loc, r4, r5)
        ),
        out_shape=jax.ShapeDtypeStruct((lanes * rows_b, wide), F32),
        in_specs=[vmem, pl.BlockSpec(memory_space=pl.ANY)] + [vmem] * 4,
        out_specs=pl.BlockSpec(memory_space=pl.ANY),
        scratch_shapes=[pltpu.VMEM(shape, F32) for shape in buffers(chunks)]
        + [
            pltpu.VMEM((nx, kx_loc, r3), F32),
            pltpu.VMEM((ny, ky_loc, r4), F32),
            pltpu.VMEM((2, 2 * b_loc * cin, nc * xl), BF16),
            pltpu.VMEM((2, ny * lanes, tu), BF16),
            pltpu.VMEM((p_loc, tu, 2 * wide), BF16),
            pltpu.VMEM((nx * nc * kx_loc, ny * 2 * p_loc), F32),
            dma,
            dma((nx,)), dma((nx,)), dma((ny,)), dma((ny,)),
            dma((chunks, nc)), dma((chunks, nc)),
            dma((chunks, nx)), dma((chunks, nx)), dma((chunks, nx)),
            dma((chunks, ny)), dma((chunks, ny)),
            dma((chunks * sub, nc)), dma((chunks * sub, nc)),
            dma((chunks * sub, nx)), dma((chunks * sub, nx + 1)),
            dma((chunks * sub,)),
            pltpu.SemaphoreType.REGULAR,
        ],
        compiler_params=pltpu.CompilerParams(
            collective_id=0, has_side_effects=True, vmem_limit_bytes=61000 * 1024
        ),
    )(
        spectrum.reshape(2 * b_loc * cin * kx_loc, lanes), core,
        input_factor.T, first_factor, second_factor, third_factor,
    )
    out = pl.pallas_call(
        functools.partial(mix, lanes),
        grid=(b_loc,),
        out_shape=jax.ShapeDtypeStruct((2, b_loc, cout * kx_loc, lanes), F32),
        in_specs=[
            pl.BlockSpec((q_all, cout), lambda b: (0, 0)),
            pl.BlockSpec((lanes * rows_b, wide), lambda b: (0, 0)),
        ],
        out_specs=pl.BlockSpec((2, 1, cout * kx_loc, lanes), lambda b: (0, b, 0, 0)),
    )(output_factor.T, fin)
    return out.reshape(2, b_loc, cout, kx_loc, lanes)


def solution(mesh):
    placed = (
        P(None, "col", None, "mx", "my"),
        P(None, "col", None, ("mx", "my"), None, None),
        P(),
        P(),
        P("mx", None),
        P("my", None),
        P(),
    )
    return jax.shard_map(
        functools.partial(
            per_device, mesh.shape["mx"], mesh.shape["my"], mesh.shape["col"]
        ),
        mesh=mesh,
        in_specs=placed,
        out_specs=P(None, "col", None, "mx", "my"),
        check_vma=False,
    )
```

time: 168 us -> 137 us (0.82); the launches traced: 166 us -> 137 us
  Pallas kernels: 163 us -> 137 us
  local copies, waits for them, and re-layouts: 3.05 us -> 0 us
    pallas_call x1, Pallas kernels: 163 us -> 133 us  [per_device(): pl.pallas_call(functools.partial(kernel, (nx, ny, nc, waves, chunks, mc,...]
    pallas_call x0 -> x1, Pallas kernels: none -> 3.76 us  [per_device(): pl.pallas_call(functools.partial(mix, lanes), grid=(b_loc,), out_shape=ja...]
    unnamed x1 -> x0, local copies, waits for them, and re-layouts: 3.05 us -> none
where the time goes in v2:
time: 137 us
  Pallas kernels  137 us (100%)
    pallas_call x1, Pallas kernels, per_device(): pl.pallas_call(functools.partial(kernel, (nx, ny, nc, waves, chunks, mc,...  133 us
    pallas_call x1, Pallas kernels, per_device(): pl.pallas_call(functools.partial(mix, lanes), grid=(b_loc,), out_shape=ja...  3.76 us

profile of v2, /device:TPU:0, one launch (start us, length us, event | category | flops | bytes accessed | tf_op | source)
XLA Modules:
  0.0 136.9 jit_solution(4962449574721619109)
XLA Ops:
  0.0 133.1 %shard_map.73.fin_ref = f32[2048,128]{1,0:T(8,128)} custom-call(f32[4096,128]{1,0:T(8,128)} %bitcast.8, f32[2,32,256,64]{3,2,1,0:T(8,128)} %bitcast.7, f32[64,128]{1,0:T(8,128)} %bitcast.9, f32[8,16]{1,0:T(8,128)} %first_ref.1, f32[8,16]{1,0:T(8,128)} %second_ref.1, f32[16,16]{1,0:T(8,128)} %third_ref.1), custom_call_target="tpu_custom_call" | custom-call | tf_op jit(solution)/shard_map/pallas_call | solution.py:570
  133.2 3.8 %shard_map.74 = f32[2,2,1024,128]{3,2,1,0:T(8,128)} custom-call(f32[64,128]{1,0:T(8,128)} %bitcast.10, f32[2048,128]{1,0:T(8,128)} %shard_map.73.fin_ref), custom_call_target="tpu_custom_call" | custom-call | tf_op jit(solution)/shard_map/pallas_call | solution.py:602

commit v3 on v2

--- a/solution.py
+++ b/solution.py
@@ -63,16 +63,16 @@
 
 def kernel(
     dims,
-    spec_ref, core_hbm, ift_ref, first_ref, second_ref, third_ref,
+    spec_hbm, core_hbm, ift_ref, first_ref, second_ref, third_ref,
     FIN,
-    core_v, XS, XA, E, C, Y, RX, ZR, F1, F2, xw, km, ready, fp,
-    core_sem, fsend, frecv, hsend, hrecv,
+    core_v, spec_ref, XS, XA, E, C, Y, RX, ZR, F1, F2, xw, km, ready, fp,
+    core_sem, spec_sem, fsend, frecv, hsend, hrecv,
     xsend, xrecv, usend, dsend, zxrecv, esend, erecv, ysend, yrecv, zsend, zrecv,
-    fin_sem, wave_sem,
+    fin_sem, direct_sem, last_sem, wave_sem,
 ):
-    nx, ny, nc, waves, chunks, mc, gang, sub, lag, hop, b_loc, cin, kx_loc, r4, r5 = dims
+    nx, ny, nc, waves, chunks, mc, gang, sub, lag, hop, last, direct, b_loc, cin, kx_loc, r4, r5 = dims
     mx, my, col = lax.axis_index("mx"), lax.axis_index("my"), lax.axis_index("col")
-    lanes = spec_ref.shape[1]
+    lanes = spec_hbm.shape[1]
     _, p_loc, tu, q_all = core_hbm.shape
     p_all = ift_ref.shape[0]
     ky_loc = second_ref.shape[0]
@@ -100,6 +100,8 @@
     def aligned(start, size):
         return pl.ds(pl.multiple_of(start, 8), size)
 
+    spec_copy = pltpu.make_async_copy(spec_hbm, spec_ref, spec_sem)
+    spec_copy.start()
     core_copy = pltpu.make_async_copy(core_hbm, core_v, core_sem)
     core_copy.start()
 
@@ -108,9 +110,11 @@
     def tell(sem, a, b, c):
         pl.semaphore_signal(sem, inc=1, device_id=(a, b, c), device_id_type=MESH)
 
-    each(1, nx, lambda d: tell(barrier, lax.rem(mx + d, nx), my, col))
+    def side(d):
+        return lax.rem(mx + whole_div(d, nc), nx), lax.rem(col + whole_rem(d, nc), nc)
+
+    each(1, nx * nc, lambda d: tell(barrier, side(d)[0], my, side(d)[1]))
     each(1, ny, lambda d: tell(barrier, mx, lax.rem(my + d, ny), col))
-    each(1, nc, lambda d: tell(barrier, mx, my, lax.rem(col + d, nc)))
 
     def first_copy(d):
         return send(first_ref, F1.at[mx], fsend.at[d], frecv.at[d], lax.rem(mx + d, nx), my, col)
@@ -131,28 +135,32 @@
 
     def x_copy(w, j, d):
         c = lax.rem(col + d, nc)
-        return send(XS.at[xs_rows(w, j, c)], XA.at[mx, j, col], xsend.at[j, d], xrecv.at[j, d], mx, my, c)
-
-    def x_arrival(w, j, d):
-        c = lax.rem(col + nc - d, nc)
-        return send(XS.at[xs_rows(w, j, c)], XA.at[mx, j, c], xsend.at[j, d], xrecv.at[j, d], mx, my, c)
+        return send(XS.at[xs_rows(w, j, c)], XA.at[mx, j, col], xsend.at[d], xrecv.at[j], mx, my, c)
+
+    def x_arrival(j):
+        landed = XA.at[mx, j, pl.ds(0, nc - 1)]
+        return send(landed, landed, xsend.at[1], xrecv.at[j], mx, my, lax.rem(col + 1, nc))
+
+    def x_direct(w, j, d):
+        a, c = side(d)
+        return send(XS.at[xs_rows(w, j, c)], XA.at[mx, j, col], direct_sem, zxrecv.at[j, mx], a, my, c)
 
     def x_up(j, g):
-        return send(XA.at[g, j], XA.at[g, j], usend.at[j, g], zxrecv.at[j, g], mx + 1, my, col)
+        return send(XA.at[g, j], XA.at[g, j], usend.at[g], zxrecv.at[whole_rem(j, zxrecv.shape[0]), g], mx + 1, my, col)
 
     def x_down(j, g):
-        return send(XA.at[g, j], XA.at[g, j], dsend.at[j, g], zxrecv.at[j, g], mx - 1, my, col)
+        return send(XA.at[g, j], XA.at[g, j], dsend.at[g], zxrecv.at[whole_rem(j, zxrecv.shape[0]), g], mx - 1, my, col)
 
     def c_rows(j, s):
         return aligned((j * ny + s) * (p_loc * mc), p_loc * mc)
 
     def e_copy(j, d):
         b = lax.rem(my + d, ny)
-        return send(E.at[j, b], C.at[c_rows(j, my)], esend.at[j, d], erecv.at[j, d], mx, b, col)
-
-    def e_arrival(j, d):
-        b = lax.rem(my + ny - d, ny)
-        return send(E.at[j, my], C.at[c_rows(j, b)], esend.at[j, d], erecv.at[j, d], mx, b, col)
+        return send(E.at[j, b], C.at[c_rows(j, my)], esend.at[d], erecv.at[j], mx, b, col)
+
+    def e_arrival(j):
+        landed = C.at[aligned(j * ny * p_loc * mc, (ny - 1) * p_loc * mc)]
+        return send(landed, landed, esend.at[1], erecv.at[j], mx, lax.rem(my + 1, ny), col)
 
     def y_row(j, c, g):
         return ((j * nc + c) * nx + g) * (my_modes * rows_b)
@@ -161,20 +169,20 @@
         c = lax.rem(col + d, nc)
         return send(
             Y.at[aligned(y_row(j, c, 0), nx * my_modes * rows_b)], RX.at[j, d - 1],
-            ysend.at[j, d], yrecv.at[j, d], mx, my, c,
+            ysend.at[d], yrecv.at[whole_rem(j, yrecv.shape[0]), d - 1], mx, my, c,
         )
 
     def y_arrival(j, d):
         c = lax.rem(col + nc - d, nc)
         return send(
             Y.at[aligned(y_row(j, c, 0), nx * my_modes * rows_b)], RX.at[j, d - 1],
-            ysend.at[j, d], yrecv.at[j, d], mx, my, c,
+            ysend.at[d], yrecv.at[whole_rem(j, yrecv.shape[0]), d - 1], mx, my, c,
         )
 
     def z_move(j, g, slot, a):
         return send(
             Y.at[aligned(y_row(j, col, g), my_modes * rows_b)], ZR.at[j, slot],
-            zsend.at[j, g], zrecv.at[j, slot], a, my, col,
+            zsend.at[g], zrecv.at[whole_rem(j, zrecv.shape[0]), slot], a, my, col,
         )
 
     def fin_copy(w, t):
@@ -182,7 +190,7 @@
         return pltpu.make_async_copy(
             Y.at[aligned(y_row(t, col, mx), rows)],
             FIN.at[aligned((w * chunks * sub + t) * rows, rows)],
-            fin_sem.at[t],
+            fin_sem,
         )
 
     n, m = 2 * b_loc * cin, nc * xl
@@ -207,7 +215,8 @@
             XS[pl.ds(c * lanes * kx_loc + k, lanes, stride=kx_loc), :] = got[:, c * xl : (c + 1) * xl]
         return 0
 
-    lax.fori_loop(0, kx_loc, rank, 0)
+    spec_copy.wait()
+    lax.fori_loop(0, kx_loc, rank, 0, unroll=4)
     by_third = exact(third_ref[...], picks_columns(r5, tu, lambda j: whole_rem(j, r5)), PLAIN)
 
     def start_spectrum(w):
@@ -216,11 +225,17 @@
             XA[mx, j, col] = XS[xs_rows(w, j, col), :]
             return 0
 
-        lax.fori_loop(0, chunks, go, 0)
+        if isinstance(w, int):
+            for j in range(direct):
+                go(j, 0)
+                each(nc, nx * nc, lambda d: x_direct(w, j, d).start())
+            lax.fori_loop(direct, chunks, go, 0)
+        else:
+            lax.fori_loop(0, chunks, go, 0)
 
     F1[mx] = first_ref[...]
     F2[my] = second_ref[...]
-    pl.semaphore_wait(barrier, nx - 1 + ny - 1 + nc - 1)
+    pl.semaphore_wait(barrier, nx * nc - 1 + ny - 1)
     each(1, ny, lambda d: second_copy(d).start())
     each(1, nx, lambda d: first_copy(d).start())
     start_spectrum(0)
@@ -232,38 +247,44 @@
         )
         return 0
 
-    lax.fori_loop(0, p_loc, prepare, 0, unroll=2)
+    lax.fori_loop(0, p_loc, prepare, 0, unroll=8)
     each(1, ny, lambda d: second_arrival(d).wait_recv())
     by_second = exact(
         F2[...].reshape(ny * ky_loc, r4),
         picks_columns(r4, tu, lambda j: whole_div(j, r5)),
         PLAIN,
     )
-    assert modes_third % mc == 0 and ny % 2 == 0
+    assert modes_third % mc == 0 and ny * mc % 16 == 0
     for j in range(lanes // mc):
         k = j * mc % modes_third
-        for b in range(0, ny, 2):
-            r = [(b + i) * ky_loc + j * mc // modes_third for i in range(2)]
+        for b in range(0, ny, 16 // mc):
+            r = [(b + i) * ky_loc + j * mc // modes_third for i in range(16 // mc)]
             tile = jnp.concatenate(
                 [by_second[i : i + 1, :] * by_third[k : k + mc, :] for i in r], axis=0
             )
-            km[0, (j * ny + b) * mc : (j * ny + b + 2) * mc, :], km[1, (j * ny + b) * mc : (j * ny + b + 2) * mc, :] = halves(tile)
+            r = (j * ny + b) * mc
+            km[0, r : r + 16, :], km[1, r : r + 16, :] = halves(tile)
 
     def expand(w, k):
         rows = gang * ny * mc
         start = pl.multiple_of((w * chunks + k * gang) * ny * mc, rows)
         left = jnp.concatenate([km[0, pl.ds(start, rows), :], km[1, pl.ds(start, rows), :]], axis=0)
 
-        def one(p, _):
-            got = plain(left, ready[p], PLAIN)
-            got = got[:rows, :wide] + (got[:rows, wide:] + got[rows:, :wide])
+        def one(t, _):
+            parts = []
+            for i in range(8 // mc):
+                got = plain(left, ready[t * (8 // mc) + i], PLAIN)
+                parts.append(got[:rows, :wide] + (got[:rows, wide:] + got[rows:, :wide]))
             for i in range(gang):
                 for b in range(ny):
                     r = (i * ny + b) * mc
-                    E[k * gang + i, b, aligned(p * mc, mc), :] = got[r : r + mc]
+                    E[k * gang + i, b, aligned(t * 8, 8), :] = jnp.concatenate(
+                        [part[r : r + mc] for part in parts], axis=0
+                    )
             return 0
 
-        lax.fori_loop(0, p_loc, one, 0, unroll=4)
+        steps = p_loc * mc // 8
+        lax.fori_loop(0, steps, one, 0, unroll=min(8, steps))
 
         def go(i, _):
             j = k * gang + i
@@ -315,12 +336,20 @@
                         Y[aligned(y_row(t, c, g) + i * rows_b + b * kx_loc, kx_loc), :] = got[r : r + kx_loc]
             return 0
 
-        lax.fori_loop(0, my_modes, one, 0, unroll=2)
+        lax.fori_loop(0, my_modes, one, 0, unroll=4)
+
+    def is_direct(w, j):
+        return isinstance(w, int) and isinstance(j, int) and j < direct
+
+    def relayed(w, j):
+        return j >= direct if isinstance(w, int) else j >= 0
 
     def spectrum_out(w, j):
         @pl.when(j < chunks)
         def _():
-            each(1, nc, lambda d: x_arrival(w, j, d).wait_recv())
+            x_arrival(j).wait_recv()
+            if is_direct(w, j):
+                return
 
             @pl.when(mx < nx - 1)
             def _():
@@ -330,14 +359,14 @@
             def _():
                 x_down(j, mx).start()
 
-    def spectrum_on(j, h):
+    def spectrum_on(w, j, h):
         @pl.when(j < chunks)
         def _():
             @pl.when(mx >= h)
             def _():
                 x_up(j, mx - h).wait_recv()
 
-                @pl.when(mx < nx - 1)
+                @pl.when((mx < nx - 1) & relayed(w, j))
                 def _():
                     x_up(j, mx - h).start()
 
@@ -345,7 +374,7 @@
             def _():
                 x_down(j, mx + h).wait_recv()
 
-                @pl.when(mx > 0)
+                @pl.when((mx > 0) & relayed(w, j))
                 def _():
                     x_down(j, mx + h).start()
 
@@ -356,9 +385,12 @@
 
     def lead(w):
         for step in range(nx - 1):
-            spectrum_out(w, step)
+            for j in range(2 * step, 2 * step + 2):
+                spectrum_out(w, j)
             for h in range(1, step + 1):
-                spectrum_on(step - h, h)
+                for j in range(2 * (step - h), 2 * (step - h) + 2):
+                    if not is_direct(w, j):
+                        spectrum_on(w, j, h)
             if step < nx - 2:
                 expand_if(w, step)
             if step == 0 and isinstance(w, int):
@@ -366,6 +398,15 @@
 
     def wave(w):
         total = chunks * sub
+
+        def z_direct(t, g):
+            return send(
+                Y.at[aligned(y_row(t, col, g), my_modes * rows_b)], ZR.at[t, z_slot(mx, g)],
+                zsend.at[g], last_sem.at[t - (total - last)], g, my, col,
+            )
+
+        def z_slot(a, g):
+            return whole_rem(a - g - 1 + nx, nx)
 
         def later(t):
             j = t - lag
@@ -385,9 +426,13 @@
 
                 lax.fori_loop(0, nx, add, 0)
 
+                @pl.when(j >= total - last)
+                def _():
+                    each(1, nx, lambda d: z_direct(j, lax.rem(mx + d, nx)).start())
+
             up = t - lag - hop * mx
 
-            @pl.when((up >= 0) & (up < total))
+            @pl.when((up >= 0) & (up < total - last))
             def _():
                 for g in range(nx - 1, -1, -1):
                     @pl.when((mx > 0) & (g >= mx))
@@ -402,7 +447,7 @@
 
             down = t - lag - hop * (nx - 1 - mx)
 
-            @pl.when((down >= 0) & (down < total))
+            @pl.when((down >= 0) & (down < total - last))
             def _():
                 for g in range(nx):
                     @pl.when((mx < nx - 1) & (g <= mx))
@@ -416,19 +461,22 @@
 
             done = t - lag - hop * jnp.maximum(mx, nx - 1 - mx)
 
-            @pl.when((done >= 0) & (done < total))
+            @pl.when((done >= 0) & (done < total - last))
             def _():
                 fin_copy(w, done).start()
 
         def tick(j, _):
-            expand_if(w, j + nx - 2)
-            spectrum_out(w, j + nx - 1)
-            for h in range(1, nx):
-                spectrum_on(j + nx - 1 - h, h)
-
             @pl.when(j < chunks)
             def _():
-                each(1, ny, lambda d: e_arrival(j, d).wait_recv())
+                e_arrival(j).wait_recv()
+
+            if isinstance(w, int):
+                @pl.when(j < direct)
+                def _():
+                    for h in range(1, nx - 1):
+                        spectrum_on(w, j, h)
+
+            spectrum_on(w, j, nx - 1)
 
             def part(u, _):
                 t = j * sub + u
@@ -438,61 +486,72 @@
                     contract(t)
                     each(1, nc, lambda d: y_copy(t, d).start())
 
-                later(t)
                 return 0
 
+            def part_later(u, _):
+                later(j * sub + u)
+                return 0
+
             lax.fori_loop(0, sub, part, 0)
+            expand_if(w, j + nx - 2)
+            spectrum_out(w, j + 2 * (nx - 1))
+            for h in range(1, nx - 1):
+                spectrum_on(w, j + 2 * (nx - 1 - h), h)
+            lax.fori_loop(0, sub, part_later, 0)
             return 0
 
         lax.fori_loop(0, chunks + -(-(lag + hop * (nx - 1)) // sub), tick, 0)
 
-        def finish(j, _):
-            each(1, nc, lambda d: x_copy(w, j, d).wait_send())
-            each(1, ny, lambda d: e_copy(j, d).wait_send())
-            for g in range(nx):
-                @pl.when((g <= mx) & (mx < nx - 1))
-                def _():
-                    x_up(j, g).wait_send()
-
-                @pl.when((g >= mx) & (mx > 0))
-                def _():
-                    x_down(j, g).wait_send()
-
-            return 0
-
-        def finish_part(t, _):
-            each(1, nc, lambda d: y_copy(t, d).wait_send())
-            for g in range(nx):
-                @pl.when(g > mx)
-                def _():
-                    z_move(t, g, g, mx + 1).wait_send()
-
-                @pl.when(g < mx)
-                def _():
-                    z_move(t, g, g, mx - 1).wait_send()
-
-            fin_copy(w, t).wait()
-            return 0
-
-        lax.fori_loop(0, chunks, finish, 0)
-        lax.fori_loop(0, total, finish_part, 0)
+        for t in range(total - last, total):
+            landed = ZR.at[t, pl.ds(0, nx - 1)]
+            send(landed, landed, zsend.at[0], last_sem.at[t - (total - last)], lax.rem(mx + 1, nx), my, col).wait_recv()
+            rows = aligned(y_row(t, col, mx), my_modes * rows_b)
+            own = Y[rows, :]
+            for d in range(nx - 1):
+                own = own + ZR[t, d]
+            Y[rows, :] = own
+            fin_copy(w, t).start()
+        first = direct if isinstance(w, int) else 0
+        if first:
+            ahead = XS.at[pl.ds(0, direct * (nx - 1) * nc * piece)]
+            send(ahead, ahead, direct_sem, direct_sem, lax.rem(mx + 1, nx), my, col).wait_send()
+
+        def sent(ref, sem, a, b, c):
+            send(ref, ref, sem, sem, a, b, c).wait_send()
+
+        each(1, nc, lambda d: sent(XS.at[pl.ds(0, chunks * piece)], xsend.at[d], mx, my, lax.rem(col + d, nc)))
+        each(1, ny, lambda d: sent(C.at[pl.ds(0, chunks * p_loc * mc)], esend.at[d], mx, lax.rem(my + d, ny), col))
+        size = total * my_modes * rows_b
+        each(1, nc, lambda d: sent(Y.at[pl.ds(0, nx * size)], ysend.at[d], mx, my, lax.rem(col + d, nc)))
+        for g in range(nx):
+            @pl.when((g <= mx) & (mx < nx - 1))
+            def _():
+                sent(XA.at[g, first:], usend.at[g], mx + 1, my, col)
+
+            @pl.when((g >= mx) & (mx > 0))
+            def _():
+                sent(XA.at[g, first:], dsend.at[g], mx - 1, my, col)
+
+            @pl.when(g > mx)
+            def _():
+                sent(Y.at[pl.ds(0, size)], zsend.at[g], mx + 1, my, col)
+
+            @pl.when(g < mx)
+            def _():
+                sent(Y.at[pl.ds(0, size)], zsend.at[g], mx - 1, my, col)
+
+        pltpu.make_async_copy(
+            Y.at[pl.ds(0, size)], FIN.at[aligned(w * size, size)], fin_sem
+        ).wait()
 
     lead(0)
     wave(0)
     if waves > 1:
         def again(w, _):
-            @pl.when(mx < nx - 1)
-            def _():
-                tell(wave_sem, mx + 1, my, col)
-
-            @pl.when(mx > 0)
-            def _():
-                tell(wave_sem, mx - 1, my, col)
-
+            each(1, nx, lambda d: tell(wave_sem, lax.rem(mx + d, nx), my, col))
             each(1, ny, lambda d: tell(wave_sem, mx, lax.rem(my + d, ny), col))
             each(1, nc, lambda d: tell(wave_sem, mx, my, lax.rem(col + d, nc)))
-            near = (mx < nx - 1).astype(jnp.int32) + (mx > 0).astype(jnp.int32)
-            pl.semaphore_wait(wave_sem, near + ny - 1 + nc - 1)
+            pl.semaphore_wait(wave_sem, nx - 1 + ny - 1 + nc - 1)
             start_spectrum(w)
             lead(w)
             wave(w)
@@ -516,11 +575,18 @@
             [jnp.concatenate([oft, none], axis=1), jnp.concatenate([none, oft], axis=1)], axis=0
         )
     )
-    for k in range(kx_loc):
-        rows = pl.ds(first + k, lanes, stride=rows_b)
-        got = dot_split(ob, halves(fin_ref[rows, :]), TURNED)
-        for c in range(2):
-            out_ref[c, 0, pl.ds(k, cout, stride=kx_loc), :] = got[c * cout : (c + 1) * cout]
+    stacked = jnp.concatenate(ob, axis=1)
+    for k in range(0, kx_loc, 2):
+        pair = [fin_ref[pl.ds(first + k + i, lanes, stride=rows_b), :] for i in range(2)]
+        high, low = halves(jnp.concatenate(pair, axis=0))
+        got = plain(stacked, jnp.concatenate([high, high], axis=1), TURNED) + plain(
+            ob[0], low, TURNED
+        )
+        for i in range(2):
+            for c in range(2):
+                out_ref[c, 0, pl.ds(k + i, cout, stride=kx_loc), :] = got[
+                    c * cout : (c + 1) * cout, i * lanes : (i + 1) * lanes
+                ]
 
 
 def per_device(
@@ -534,7 +600,7 @@
     ky_loc = second_factor.shape[0]
     assert r3 == nx * ny
     tu = r4 * r5
-    mc, sub, lag, hop = 8, 2, 2, 3
+    mc, sub, lag, hop, last = 4, 1, 2, 2, 6
     xl = -(-(b_loc * 2 * p_loc) // 128) * 128
     rows_b = b_loc * kx_loc
     wide = 2 * q_all
@@ -542,6 +608,7 @@
     def buffers(chunks):
         return [
             (2, p_loc, tu, q_all),
+            (2 * b_loc * cin * kx_loc, lanes),
             (nc * lanes * kx_loc, xl),
             (nx, chunks, nc, mc * kx_loc, xl),
             (chunks, ny, p_loc * mc, wide),
@@ -558,10 +625,11 @@
         return size
 
     waves = 1
-    fixed = 4 * lanes * rows_b * 2 * cin + 4 * p_loc * tu * wide
+    fixed = 4 * p_loc * tu * wide
     while fixed + sum(map(held, buffers(lanes // mc // waves))) > 58 * 2**20:
         waves *= 2
     chunks = lanes // mc // waves
+    last, direct = min(last, chunks * sub), min(2, chunks)
     gang = min(chunks, max(1, 64 // (ny * mc)))
 
     core = jnp.transpose(core_tensor, (0, 1, 3, 4, 5, 2)).reshape(2, p_loc, tu, q_all)
@@ -569,10 +637,10 @@
     dma = pltpu.SemaphoreType.DMA
     fin = pl.pallas_call(
         functools.partial(
-            kernel, (nx, ny, nc, waves, chunks, mc, gang, sub, lag, hop, b_loc, cin, kx_loc, r4, r5)
+            kernel, (nx, ny, nc, waves, chunks, mc, gang, sub, lag, hop, last, direct, b_loc, cin, kx_loc, r4, r5)
         ),
         out_shape=jax.ShapeDtypeStruct((lanes * rows_b, wide), F32),
-        in_specs=[vmem, pl.BlockSpec(memory_space=pl.ANY)] + [vmem] * 4,
+        in_specs=[pl.BlockSpec(memory_space=pl.ANY)] * 2 + [vmem] * 4,
         out_specs=pl.BlockSpec(memory_space=pl.ANY),
         scratch_shapes=[pltpu.VMEM(shape, F32) for shape in buffers(chunks)]
         + [
@@ -582,14 +650,14 @@
             pltpu.VMEM((2, ny * lanes, tu), BF16),
             pltpu.VMEM((p_loc, tu, 2 * wide), BF16),
             pltpu.VMEM((nx * nc * kx_loc, ny * 2 * p_loc), F32),
-            dma,
+            dma, dma,
             dma((nx,)), dma((nx,)), dma((ny,)), dma((ny,)),
-            dma((chunks, nc)), dma((chunks, nc)),
-            dma((chunks, nx)), dma((chunks, nx)), dma((chunks, nx)),
-            dma((chunks, ny)), dma((chunks, ny)),
-            dma((chunks * sub, nc)), dma((chunks * sub, nc)),
-            dma((chunks * sub, nx)), dma((chunks * sub, nx + 1)),
-            dma((chunks * sub,)),
+            dma((nc,)), dma((chunks,)),
+            dma((nx,)), dma((nx,)), dma((min(16, chunks), nx)),
+            dma((ny,)), dma((chunks,)),
+            dma((nc,)), dma((min(8, chunks * sub), max(nc - 1, 1))),
+            dma((nx,)), dma((min(8, chunks * sub), nx + 1)),
+            dma, dma, dma((last,)),
             pltpu.SemaphoreType.REGULAR,
         ],
         compiler_params=pltpu.CompilerParams(

time: 137 us -> 125 us (0.912)
  Pallas kernels: 137 us -> 125 us
    pallas_call x1, Pallas kernels: 133 us -> 122 us  [per_device(): pl.pallas_call(functools.partial(kernel, (nx, ny, nc, waves, chunks, mc,...]
where the time goes in v3:
time: 125 us
  Pallas kernels  125 us (100%)
    pallas_call x1, Pallas kernels, per_device(): pl.pallas_call(functools.partial(kernel, (nx, ny, nc, waves, chunks, mc,...  122 us
    pallas_call x1, Pallas kernels, per_device(): pl.pallas_call(functools.partial(mix, lanes), grid=(b_loc,), out_shape=ja...  3.42 us

profile of v3, /device:TPU:0, one launch (start us, length us, event | category | flops | bytes accessed | tf_op | source)
XLA Modules:
  0.0 125.2 jit_solution(12632895590198570230)
XLA Ops:
  0.0 121.8 %shard_map.73.fin_ref = f32[2048,128]{1,0:T(8,128)} custom-call(f32[4096,128]{1,0:T(8,128)} %bitcast.8, f32[2,32,256,64]{3,2,1,0:T(8,128)} %bitcast.7, f32[64,128]{1,0:T(8,128)} %bitcast.9, f32[8,16]{1,0:T(8,128)} %first_ref.1, f32[8,16]{1,0:T(8,128)} %second_ref.1, f32[16,16]{1,0:T(8,128)} %third_ref.1), custom_call_target="tpu_custom_call" | custom-call | tf_op jit(solution)/shard_map/pallas_call | solution.py:638
  121.8 3.4 %shard_map.74 = f32[2,2,1024,128]{3,2,1,0:T(8,128)} custom-call(f32[64,128]{1,0:T(8,128)} %bitcast.10, f32[2048,128]{1,0:T(8,128)} %shard_map.73.fin_ref), custom_call_target="tpu_custom_call" | custom-call | tf_op jit(solution)/shard_map/pallas_call | solution.py:670

commit v4 on v3

--- a/solution.py
+++ b/solution.py
@@ -100,10 +100,19 @@
     def aligned(start, size):
         return pl.ds(pl.multiple_of(start, 8), size)
 
-    spec_copy = pltpu.make_async_copy(spec_hbm, spec_ref, spec_sem)
-    spec_copy.start()
-    core_copy = pltpu.make_async_copy(core_hbm, core_v, core_sem)
-    core_copy.start()
+    spec_rows, core_rows = spec_hbm.shape[0] // spec_sem.shape[0], p_loc // core_sem.shape[1]
+
+    def spec_copy(i):
+        rows = aligned(i * spec_rows, spec_rows)
+        return pltpu.make_async_copy(spec_hbm.at[rows], spec_ref.at[rows], spec_sem.at[i])
+
+    def core_copy(c, i):
+        rows = pl.ds(i * core_rows, core_rows)
+        return pltpu.make_async_copy(core_hbm.at[c, rows], core_v.at[c, rows], core_sem.at[c, i])
+
+    each(0, spec_sem.shape[0], lambda i: spec_copy(i).start())
+    for c in range(2):
+        each(0, core_sem.shape[1], lambda i: core_copy(c, i).start())
 
     barrier = pltpu.get_barrier_semaphore()
 
@@ -215,7 +224,7 @@
             XS[pl.ds(c * lanes * kx_loc + k, lanes, stride=kx_loc), :] = got[:, c * xl : (c + 1) * xl]
         return 0
 
-    spec_copy.wait()
+    each(0, spec_sem.shape[0], lambda i: spec_copy(i).wait())
     lax.fori_loop(0, kx_loc, rank, 0, unroll=4)
     by_third = exact(third_ref[...], picks_columns(r5, tu, lambda j: whole_rem(j, r5)), PLAIN)
 
@@ -239,7 +248,8 @@
     each(1, ny, lambda d: second_copy(d).start())
     each(1, nx, lambda d: first_copy(d).start())
     start_spectrum(0)
-    core_copy.wait()
+    for c in range(2):
+        each(0, core_sem.shape[1], lambda i: core_copy(c, i).wait())
 
     def prepare(p, _):
         ready[p, :, :wide], ready[p, :, wide:] = halves(
@@ -629,7 +639,7 @@
     while fixed + sum(map(held, buffers(lanes // mc // waves))) > 58 * 2**20:
         waves *= 2
     chunks = lanes // mc // waves
-    last, direct = min(last, chunks * sub), min(2, chunks)
+    last, direct = min(last, chunks * sub), min(1, chunks)
     gang = min(chunks, max(1, 64 // (ny * mc)))
 
     core = jnp.transpose(core_tensor, (0, 1, 3, 4, 5, 2)).reshape(2, p_loc, tu, q_all)
@@ -650,7 +660,7 @@
             pltpu.VMEM((2, ny * lanes, tu), BF16),
             pltpu.VMEM((p_loc, tu, 2 * wide), BF16),
             pltpu.VMEM((nx * nc * kx_loc, ny * 2 * p_loc), F32),
-            dma, dma,
+            dma((2, 4)), dma((4,)),
             dma((nx,)), dma((nx,)), dma((ny,)), dma((ny,)),
             dma((nc,)), dma((chunks,)),
             dma((nx,)), dma((nx,)), dma((min(16, chunks), nx)),

time: 125 us -> 124 us (level)
  no operation moved by 1% of the time
where the time goes in v4:
time: 124 us
  Pallas kernels  124 us (100%)
    pallas_call x1, Pallas kernels, per_device(): pl.pallas_call(functools.partial(kernel, (nx, ny, nc, waves, chunks, mc,...  121 us
    pallas_call x1, Pallas kernels, per_device(): pl.pallas_call(functools.partial(mix, lanes), grid=(b_loc,), out_shape=ja...  3.42 us

profile of v4, /device:TPU:0, one launch (start us, length us, event | category | flops | bytes accessed | tf_op | source)
XLA Modules:
  0.0 124.2 jit_solution(8473094066237640738)
XLA Ops:
  0.0 120.8 %shard_map.73.fin_ref = f32[2048,128]{1,0:T(8,128)} custom-call(f32[4096,128]{1,0:T(8,128)} %bitcast.8, f32[2,32,256,64]{3,2,1,0:T(8,128)} %bitcast.7, f32[64,128]{1,0:T(8,128)} %bitcast.9, f32[8,16]{1,0:T(8,128)} %first_ref.1, f32[8,16]{1,0:T(8,128)} %second_ref.1, f32[16,16]{1,0:T(8,128)} %third_ref.1), custom_call_target="tpu_custom_call" | custom-call | tf_op jit(solution)/shard_map/pallas_call | solution.py:648
  120.8 3.4 %shard_map.74 = f32[2,2,1024,128]{3,2,1,0:T(8,128)} custom-call(f32[64,128]{1,0:T(8,128)} %bitcast.10, f32[2048,128]{1,0:T(8,128)} %shard_map.73.fin_ref), custom_call_target="tpu_custom_call" | custom-call | tf_op jit(solution)/shard_map/pallas_call | solution.py:680

commit v5 on v4

--- a/solution.py
+++ b/solution.py
@@ -503,10 +503,10 @@
                 return 0
 
             lax.fori_loop(0, sub, part, 0)
-            expand_if(w, j + nx - 2)
             spectrum_out(w, j + 2 * (nx - 1))
             for h in range(1, nx - 1):
                 spectrum_on(w, j + 2 * (nx - 1 - h), h)
+            expand_if(w, j + nx - 2)
             lax.fori_loop(0, sub, part_later, 0)
             return 0
 
@@ -610,7 +610,7 @@
     ky_loc = second_factor.shape[0]
     assert r3 == nx * ny
     tu = r4 * r5
-    mc, sub, lag, hop, last = 4, 1, 2, 2, 6
+    mc, sub, lag, hop, last = 4, 1, 2, 2, 5
     xl = -(-(b_loc * 2 * p_loc) // 128) * 128
     rows_b = b_loc * kx_loc
     wide = 2 * q_all
@@ -660,7 +660,7 @@
             pltpu.VMEM((2, ny * lanes, tu), BF16),
             pltpu.VMEM((p_loc, tu, 2 * wide), BF16),
             pltpu.VMEM((nx * nc * kx_loc, ny * 2 * p_loc), F32),
-            dma((2, 4)), dma((4,)),
+            dma((2, 1)), dma((1,)),
             dma((nx,)), dma((nx,)), dma((ny,)), dma((ny,)),
             dma((nc,)), dma((chunks,)),
             dma((nx,)), dma((nx,)), dma((min(16, chunks), nx)),

time: 124 us -> 126 us (1.016)
  no operation moved by 1% of the time
where the time goes in v5:
time: 126 us; the launch traced here: 125 us
  Pallas kernels  125 us (99%)
    pallas_call x1, Pallas kernels, per_device(): pl.pallas_call(functools.partial(kernel, (nx, ny, nc, waves, chunks, mc,...  122 us
    pallas_call x1, Pallas kernels, per_device(): pl.pallas_call(functools.partial(mix, lanes), grid=(b_loc,), out_shape=ja...  3.42 us

profile of v5, /device:TPU:0, one launch (start us, length us, event | category | flops | bytes accessed | tf_op | source)
XLA Modules:
  0.0 125.5 jit_solution(4068125251468566218)
XLA Ops:
  0.0 122.0 %shard_map.73.fin_ref = f32[2048,128]{1,0:T(8,128)} custom-call(f32[4096,128]{1,0:T(8,128)} %bitcast.8, f32[2,32,256,64]{3,2,1,0:T(8,128)} %bitcast.7, f32[64,128]{1,0:T(8,128)} %bitcast.9, f32[8,16]{1,0:T(8,128)} %first_ref.1, f32[8,16]{1,0:T(8,128)} %second_ref.1, f32[16,16]{1,0:T(8,128)} %third_ref.1), custom_call_target="tpu_custom_call" | custom-call | tf_op jit(solution)/shard_map/pallas_call | solution.py:648
  122.0 3.4 %shard_map.74 = f32[2,2,1024,128]{3,2,1,0:T(8,128)} custom-call(f32[64,128]{1,0:T(8,128)} %bitcast.10, f32[2048,128]{1,0:T(8,128)} %shard_map.73.fin_ref), custom_call_target="tpu_custom_call" | custom-call | tf_op jit(solution)/shard_map/pallas_call | solution.py:680
